TPU v7x, 512 devices: a whole 4x8x8 slice. The times are simulated.
512 devices in a mesh: rows: 64 (over y, z), inner: 8 (over x, core).
Axes of the slice: x: 4, y: 8, z: 8, core: 2. Of those that a mesh axis runs over, the one named last changes fastest.
Arguments:
- r_tiles: bfloat16 [512, 64, 128, 128], P('rows', 'inner'), may hold values from -0.5 to 0.5
- r_cols: int32 [512, 64], P('rows', 'inner'), may hold values from 0 to 4095, as said below
- a_tiles: bfloat16 [4096, 7, 128, 128], P(('rows', 'inner')), may hold values from -6 to 6
- a_cols: int32 [4096, 7], replicated, may hold values from 0 to 4095, as said below
- c_cols: int32 [512, 8], P('rows'), may hold values from -1 to 4095, as said below
- c_counts: int32 [512], P('rows'), may hold values from 4 to 8, as said below
Outputs:
- c_tiles: bfloat16 [512, 8, 128, 128], P('rows', 'inner')
- row_offsets: int32 [512], P('rows')
Inputs may be any that keep to these rules, and one draw needn't show every extreme that they name: `r_cols`: the slots g * 8 to (g + 1) * 8 - 1 of block row c name distinct fine block rows k with (k // 8) % 8 == g and k // 64 within one of c // 8. `a_cols`: row k names 7 distinct fine block columns, the first of them k. `c_cols`: the first c_counts[c] entries of row c are distinct block columns, the others are -1. `c_counts`: each aligned group of 8 block rows has one with 8 live slots.
All inputs are finite; a program needn't handle non-finite values.
Results may differ from a plain program's by a relative error of at most 0.001.
Values may be sent and summed in bfloat16 or wider, within the bound.
No kernel may reach another device: no remote copies, remote signals or barrier semaphores. Data moves between devices by JAX's collectives and lax.ppermute only.
A program may use at most 64 MiB of HBM per device.

v0:
```python
import jax
import jax.numpy as jnp
from jax import lax
from jax.sharding import Mesh
from jax.sharding import PartitionSpec as P

ROWS = ("rows_0", "rows_1")
ROWS_INNER = ("rows_0", "rows_1", "inner")


def padded(block, sides, width):
    for axis, dim in sides:
        count = lax.axis_size(axis)
        forward = [(i, i + 1) for i in range(count - 1)]
        backward = [(target, source) for source, target in forward]
        low = lax.ppermute(
            lax.slice_in_dim(block, block.shape[dim] - width, None, axis=dim), axis, forward
        )
        high = lax.ppermute(lax.slice_in_dim(block, 0, width, axis=dim), axis, backward)
        block = jnp.concatenate([low, block, high], axis=dim)
    return block


def split_up(value, dim, size):
    lengths = value.shape
    parts = value.reshape(*lengths[:dim], size, lengths[dim] // size, *lengths[dim + 1 :])
    return jnp.moveaxis(parts, dim, 0)


def sent_and_summed(value, axis, dim):
    size = lax.axis_size(axis)
    parts = lax.all_to_all(split_up(value, dim, size), axis, 0, 0, tiled=True)
    return jnp.sum(parts, axis=0)


def in_order(parts, dim):
    parts = jnp.moveaxis(parts, 0, dim)
    lengths = parts.shape
    return parts.reshape(*lengths[:dim], lengths[dim] * lengths[dim + 1], *lengths[dim + 2 :])


def all_blocks(value, axes, order):
    parts = value[None]
    for k in order:
        parts = lax.all_gather(parts, axes[k], axis=0, tiled=True)
    block = [lax.axis_size(axes[k]) for k in reversed(order)]
    parts = parts.reshape(*block, *value.shape)
    turned = sorted(range(len(order)), key=lambda place: order[len(order) - 1 - place])
    return parts.transpose(*turned, *range(len(order), parts.ndim)).reshape(-1, *value.shape)


def gathered_by_axis(value, axes, order, dim):
    return in_order(all_blocks(value, axes, order), dim)


def body(r_tiles, r_cols, a_tiles, a_cols, c_cols, c_counts):
    local_rows = a_tiles.shape[0]
    op_slots = a_tiles.shape[1]
    tile_size = a_tiles.shape[2]
    row_count = r_tiles.shape[0]
    r_slots = r_tiles.shape[1]
    groups = lax.axis_size("inner")
    row_index = lax.axis_index(ROWS)
    nearby = padded(a_tiles, ((ROWS, 0),), local_rows)
    halo_tiles = nearby.shape[0] * op_slots
    flat_tiles = nearby.reshape(halo_tiles, tile_size * tile_size)
    owner_rows = r_cols // local_rows // groups
    within = (owner_rows - row_index + 1) * local_rows + r_cols % local_rows
    wide_rows = jnp.transpose(r_tiles, (0, 2, 1, 3)).reshape(
        row_count, tile_size, r_slots * tile_size
    )
    slot_ids = jnp.arange(op_slots, dtype=jnp.int32)
    tile_ids = jnp.arange(halo_tiles, dtype=jnp.int32)

    def row_partial(row_wide, halo_slot, columns, wanted):
        matches = wanted[:, None, None] == a_cols[columns][None]
        hits = jnp.sum(matches.astype(jnp.int32), axis=2)
        target = jnp.sum(
            jnp.where(matches, halo_slot[None, :, None] * op_slots + slot_ids[None, None, :], 0),
            axis=2,
        )
        selector = (
            (tile_ids[None, None, :] == target[:, :, None]) & (hits[:, :, None] > 0)
        ).astype(jnp.bfloat16)
        selector = selector.reshape(wanted.shape[0] * r_slots, halo_tiles)
        chosen = jnp.dot(selector, flat_tiles, preferred_element_type=jnp.float32).astype(
            jnp.bfloat16
        )
        chosen = chosen.reshape(wanted.shape[0], r_slots * tile_size, tile_size)
        return jnp.einsum("xm,smz->sxz", row_wide, chosen, preferred_element_type=jnp.float32)

    def one_row(unused, row_data):
        row_wide, halo_slot, columns, wanted = row_data
        return (unused, row_partial(row_wide, halo_slot, columns, wanted))

    _, partial_value = lax.scan(one_row, jnp.int32(0), (wide_rows, within, r_cols, c_cols))
    own_slots = sent_and_summed(partial_value, "inner", 1)
    c_tiles = own_slots.astype(jnp.bfloat16)
    local_total = jnp.sum(c_counts)
    totals = gathered_by_axis(local_total[None], ROWS, (0, 1), 0)
    first_offset = jnp.sum(jnp.where(jnp.arange(totals.shape[0]) < row_index, totals, 0))
    row_offsets = first_offset + jnp.cumsum(c_counts) - c_counts
    return (c_tiles, row_offsets)


def solution(mesh):
    finer = Mesh(mesh.devices.reshape(8, 8, mesh.shape["inner"]), ("rows_0", "rows_1", "inner"))
    return jax.shard_map(
        body,
        mesh=finer,
        in_specs=(
            P(ROWS, "inner", None, None),
            P(ROWS, "inner"),
            P(ROWS_INNER, None, None, None),
            P(),
            P(ROWS, None),
            P(ROWS),
        ),
        out_specs=(P(ROWS, "inner", None, None), P(ROWS)),
        check_vma=False,
    )
```

profile of v0, /device:TPU:40, one launch (start us, length us, event | category | flops | bytes accessed | tf_op | source)
XLA Modules:
  0.0 247.9 jit_solution(15802767935225193197)
XLA Ops:
  0.7 4.4 %collective-permute-start = (bf16[8,7,128,128]{3,2,1,0:T(8,128)(2,1)}, bf16[8,7,128,128]{3,2,1,0:T(8,128)(2,1)}, u32[]{:S(2)}, u32[]{:S(2)}) collective-permute-start(bf16[8,7,128,128]{3,2,1,0:T(8,128)(2,1)} %param.10), channel_id=1, source_target_pairs={{0,8},{8,16},{16,24},{24,32},{32,40},{40,48},{48,56},{56,64},{64,7... | collective-permute-start | bytes 5505032 | tf_op jit(solution)/shard_map/ppermute | solution.py:16
  5.1 9.4 %collective-permute-start.1 = (bf16[8,7,128,128]{3,2,1,0:T(8,128)(2,1)}, bf16[8,7,128,128]{3,2,1,0:T(8,128)(2,1)}, u32[]{:S(2)}, u32[]{:S(2)}) collective-permute-start(bf16[8,7,128,128]{3,2,1,0:T(8,128)(2,1)} %param.10), channel_id=1, source_target_pairs={{8,0},{16,8},{24,16},{32,24},{40,32},{48,40},{56,48},{64,56},{72,6... | collective-permute-start | bytes 5505032 | tf_op jit(solution)/shard_map/ppermute | solution.py:19
  14.5 2.9 %copy.20 = s32[4096,7]{1,0:T(8,128)} copy(s32[4096,7]{0,1:T(8,128)} %param.11) | data formatting | bytes 229376
  17.4 1.8 copy_bitcast_fusion.1
  19.2 33.7 %collective-permute-done = bf16[8,7,128,128]{3,2,1,0:T(8,128)(2,1)} collective-permute-done((bf16[8,7,128,128]{3,2,1,0:T(8,128)(2,1)}, bf16[8,7,128,128]{3,2,1,0:T(8,128)(2,1)}, u32[]{:S(2)}, u32[]{:S(2)}) %collective-permute-start) | collective-permute-done | bytes 1835040 | tf_op jit(solution)/shard_map/ppermute | solution.py:16
  52.8 1.2 collective-permute-done.1
  54.0 2.6 %pad_maximum_fusion = bf16[24,7,128,128]{3,2,1,0:T(8,128)(2,1)S(1)} fusion(bf16[8,7,128,128]{3,2,1,0:T(8,128)(2,1)} %collective-permute-done.1, bf16[8,7,128,128]{3,2,1,0:T(8,128)(2,1)S(1)} %copy-done.1, bf16[8,7,128,128]{3,2,1,0:T(8,128)(2,1)} %collective-permute-done), kind=kLoop, calls=%fused_computation.30 | loop fusion | flops 5505024 | bytes 11010048 | tf_op jit(solution)/shard_map/concatenate | solution.py:20
  56.7 7.4 %copy.33 = bf16[21,8,128,128]{3,1,2,0:T(8,128)(2,1)} copy(bf16[21,8,128,128]{3,2,1,0:T(8,128)(2,1)S(1)} %bitcast.68) | data formatting | bytes 11010048
  64.0 126.2 %while.11 = (s32[]{:T(128)}, f32[8,8,128,128]{2,3,0,1:T(8,128)}, s32[8,8]{1,0:T(8,128)}, s32[8,8]{1,0:T(8,128)S(1)}, s32[4096,7]{1,0:T(8,128)}, /*index=5*/s32[8...) while((s32[]{:T(128)}, f32[8,8,128,128]{2,3,0,1:T(8,128)}, ...), condition=%wide.region_3.4_spmd.clone, body=%wide.region_0.3_spmd.clone.sunk | while | flops 621830400 | bytes 14688965 | solution.py:96
  64.0 0.7 fusion.44
  64.8 2.1 gather_fusion
  67.3 5.2 %convolution_convert_fusion.2 = bf16[64,16384]{1,0:T(8,128)(2,1)} fusion(bf16[168,16384]{1,0:T(8,128)(2,1)} %get-tuple-element.203, s32[64]{0:T(128)S(1)} %eq.70, pred[64]{0:T(512)(128)(4,1)S(1)} %gt.17), kind=kOutput, calls=%fused_computation.3.clone.1 | convolution fusion | flops 353391616 | bytes 7602496 | tf_op jit(solution)/shard_map/while/body/eval_jaxpr/dot_general | solution.py:86
  72.4 4.2 %reshape.195 = bf16[8,1024,128]{2,1,0:T(8,128)(2,1)} reshape(bf16[64,16384]{1,0:T(8,128)(2,1)} %convolution_convert_fusion.2) | data formatting | bytes 4194304 | tf_op jit(solution)/shard_map/while/body/eval_jaxpr/reshape | solution.py:89
  76.7 3.2 %fusion.46 = f32[8,8,128,128]{2,3,0,1:T(8,128)} fusion(f32[8,8,128,128]{2,3,0,1:T(8,128)} %get-tuple-element.189, s32[]{:T(128)} %get-tuple-element.188, bf16[8,1024,128]{2,1,0:T(8,128)(2,1)} %reshape.195, bf16[8,128,1024]{2,1,0:T(8,128)(2,1)} %get-tuple-element.204), kind=kOutput, calls=%fused_computation.5.clone.1 | convolution fusion | flops 268435456 | bytes 2884608 | tf_op jit(solution)/shard_map/while/body/eval_jaxpr/xm,smz->sxz/dot_general | solution.py:90
  79.8 0.7 fusion.44
  80.5 2.1 gather_fusion
  82.9 0.1 gt.17
  83.0 5.2 %convolution_convert_fusion.2 = bf16[64,16384]{1,0:T(8,128)(2,1)} fusion(bf16[168,16384]{1,0:T(8,128)(2,1)} %get-tuple-element.203, s32[64]{0:T(128)S(1)} %eq.70, pred[64]{0:T(512)(128)(4,1)S(1)} %gt.17), kind=kOutput, calls=%fused_computation.3.clone.1 | convolution fusion | flops 353391616 | bytes 7602496 | tf_op jit(solution)/shard_map/while/body/eval_jaxpr/dot_general | solution.py:86
  88.2 4.2 %reshape.195 = bf16[8,1024,128]{2,1,0:T(8,128)(2,1)} reshape(bf16[64,16384]{1,0:T(8,128)(2,1)} %convolution_convert_fusion.2) | data formatting | bytes 4194304 | tf_op jit(solution)/shard_map/while/body/eval_jaxpr/reshape | solution.py:89
  92.4 3.2 %fusion.46 = f32[8,8,128,128]{2,3,0,1:T(8,128)} fusion(f32[8,8,128,128]{2,3,0,1:T(8,128)} %get-tuple-element.189, s32[]{:T(128)} %get-tuple-element.188, bf16[8,1024,128]{2,1,0:T(8,128)(2,1)} %reshape.195, bf16[8,128,1024]{2,1,0:T(8,128)(2,1)} %get-tuple-element.204), kind=kOutput, calls=%fused_computation.5.clone.1 | convolution fusion | flops 268435456 | bytes 2884608 | tf_op jit(solution)/shard_map/while/body/eval_jaxpr/xm,smz->sxz/dot_general | solution.py:90
  95.6 0.7 fusion.44
  96.3 2.1 gather_fusion
  98.8 5.2 %convolution_convert_fusion.2 = bf16[64,16384]{1,0:T(8,128)(2,1)} fusion(bf16[168,16384]{1,0:T(8,128)(2,1)} %get-tuple-element.203, s32[64]{0:T(128)S(1)} %eq.70, pred[64]{0:T(512)(128)(4,1)S(1)} %gt.17), kind=kOutput, calls=%fused_computation.3.clone.1 | convolution fusion | flops 353391616 | bytes 7602496 | tf_op jit(solution)/shard_map/while/body/eval_jaxpr/dot_general | solution.py:86
  104.0 4.2 %reshape.195 = bf16[8,1024,128]{2,1,0:T(8,128)(2,1)} reshape(bf16[64,16384]{1,0:T(8,128)(2,1)} %convolution_convert_fusion.2) | data formatting | bytes 4194304 | tf_op jit(solution)/shard_map/while/body/eval_jaxpr/reshape | solution.py:89
  108.2 3.1 %fusion.46 = f32[8,8,128,128]{2,3,0,1:T(8,128)} fusion(f32[8,8,128,128]{2,3,0,1:T(8,128)} %get-tuple-element.189, s32[]{:T(128)} %get-tuple-element.188, bf16[8,1024,128]{2,1,0:T(8,128)(2,1)} %reshape.195, bf16[8,128,1024]{2,1,0:T(8,128)(2,1)} %get-tuple-element.204), kind=kOutput, calls=%fused_computation.5.clone.1 | convolution fusion | flops 268435456 | bytes 2884608 | tf_op jit(solution)/shard_map/while/body/eval_jaxpr/xm,smz->sxz/dot_general | solution.py:90
  111.4 0.7 fusion.44
  112.1 2.1 gather_fusion
  114.6 5.2 %convolution_convert_fusion.2 = bf16[64,16384]{1,0:T(8,128)(2,1)} fusion(bf16[168,16384]{1,0:T(8,128)(2,1)} %get-tuple-element.203, s32[64]{0:T(128)S(1)} %eq.70, pred[64]{0:T(512)(128)(4,1)S(1)} %gt.17), kind=kOutput, calls=%fused_computation.3.clone.1 | convolution fusion | flops 353391616 | bytes 7602496 | tf_op jit(solution)/shard_map/while/body/eval_jaxpr/dot_general | solution.py:86
  119.8 4.2 %reshape.195 = bf16[8,1024,128]{2,1,0:T(8,128)(2,1)} reshape(bf16[64,16384]{1,0:T(8,128)(2,1)} %convolution_convert_fusion.2) | data formatting | bytes 4194304 | tf_op jit(solution)/shard_map/while/body/eval_jaxpr/reshape | solution.py:89
  124.0 3.2 %fusion.46 = f32[8,8,128,128]{2,3,0,1:T(8,128)} fusion(f32[8,8,128,128]{2,3,0,1:T(8,128)} %get-tuple-element.189, s32[]{:T(128)} %get-tuple-element.188, bf16[8,1024,128]{2,1,0:T(8,128)(2,1)} %reshape.195, bf16[8,128,1024]{2,1,0:T(8,128)(2,1)} %get-tuple-element.204), kind=kOutput, calls=%fused_computation.5.clone.1 | convolution fusion | flops 268435456 | bytes 2884608 | tf_op jit(solution)/shard_map/while/body/eval_jaxpr/xm,smz->sxz/dot_general | solution.py:90
  127.1 0.7 fusion.44
  127.9 2.1 gather_fusion
  130.4 5.2 %convolution_convert_fusion.2 = bf16[64,16384]{1,0:T(8,128)(2,1)} fusion(bf16[168,16384]{1,0:T(8,128)(2,1)} %get-tuple-element.203, s32[64]{0:T(128)S(1)} %eq.70, pred[64]{0:T(512)(128)(4,1)S(1)} %gt.17), kind=kOutput, calls=%fused_computation.3.clone.1 | convolution fusion | flops 353391616 | bytes 7602496 | tf_op jit(solution)/shard_map/while/body/eval_jaxpr/dot_general | solution.py:86
  135.5 4.2 %reshape.195 = bf16[8,1024,128]{2,1,0:T(8,128)(2,1)} reshape(bf16[64,16384]{1,0:T(8,128)(2,1)} %convolution_convert_fusion.2) | data formatting | bytes 4194304 | tf_op jit(solution)/shard_map/while/body/eval_jaxpr/reshape | solution.py:89
  139.8 3.2 %fusion.46 = f32[8,8,128,128]{2,3,0,1:T(8,128)} fusion(f32[8,8,128,128]{2,3,0,1:T(8,128)} %get-tuple-element.189, s32[]{:T(128)} %get-tuple-element.188, bf16[8,1024,128]{2,1,0:T(8,128)(2,1)} %reshape.195, bf16[8,128,1024]{2,1,0:T(8,128)(2,1)} %get-tuple-element.204), kind=kOutput, calls=%fused_computation.5.clone.1 | convolution fusion | flops 268435456 | bytes 2884608 | tf_op jit(solution)/shard_map/while/body/eval_jaxpr/xm,smz->sxz/dot_general | solution.py:90
  142.9 0.7 fusion.44
  143.6 2.1 gather_fusion
  146.1 5.2 %convolution_convert_fusion.2 = bf16[64,16384]{1,0:T(8,128)(2,1)} fusion(bf16[168,16384]{1,0:T(8,128)(2,1)} %get-tuple-element.203, s32[64]{0:T(128)S(1)} %eq.70, pred[64]{0:T(512)(128)(4,1)S(1)} %gt.17), kind=kOutput, calls=%fused_computation.3.clone.1 | convolution fusion | flops 353391616 | bytes 7602496 | tf_op jit(solution)/shard_map/while/body/eval_jaxpr/dot_general | solution.py:86
  151.3 4.2 %reshape.195 = bf16[8,1024,128]{2,1,0:T(8,128)(2,1)} reshape(bf16[64,16384]{1,0:T(8,128)(2,1)} %convolution_convert_fusion.2) | data formatting | bytes 4194304 | tf_op jit(solution)/shard_map/while/body/eval_jaxpr/reshape | solution.py:89
  155.5 3.1 %fusion.46 = f32[8,8,128,128]{2,3,0,1:T(8,128)} fusion(f32[8,8,128,128]{2,3,0,1:T(8,128)} %get-tuple-element.189, s32[]{:T(128)} %get-tuple-element.188, bf16[8,1024,128]{2,1,0:T(8,128)(2,1)} %reshape.195, bf16[8,128,1024]{2,1,0:T(8,128)(2,1)} %get-tuple-element.204), kind=kOutput, calls=%fused_computation.5.clone.1 | convolution fusion | flops 268435456 | bytes 2884608 | tf_op jit(solution)/shard_map/while/body/eval_jaxpr/xm,smz->sxz/dot_general | solution.py:90
  158.7 0.7 fusion.44
  159.4 2.1 gather_fusion
  161.9 5.2 %convolution_convert_fusion.2 = bf16[64,16384]{1,0:T(8,128)(2,1)} fusion(bf16[168,16384]{1,0:T(8,128)(2,1)} %get-tuple-element.203, s32[64]{0:T(128)S(1)} %eq.70, pred[64]{0:T(512)(128)(4,1)S(1)} %gt.17), kind=kOutput, calls=%fused_computation.3.clone.1 | convolution fusion | flops 353391616 | bytes 7602496 | tf_op jit(solution)/shard_map/while/body/eval_jaxpr/dot_general | solution.py:86
  167.1 4.2 %reshape.195 = bf16[8,1024,128]{2,1,0:T(8,128)(2,1)} reshape(bf16[64,16384]{1,0:T(8,128)(2,1)} %convolution_convert_fusion.2) | data formatting | bytes 4194304 | tf_op jit(solution)/shard_map/while/body/eval_jaxpr/reshape | solution.py:89
  171.3 3.1 %fusion.46 = f32[8,8,128,128]{2,3,0,1:T(8,128)} fusion(f32[8,8,128,128]{2,3,0,1:T(8,128)} %get-tuple-element.189, s32[]{:T(128)} %get-tuple-element.188, bf16[8,1024,128]{2,1,0:T(8,128)(2,1)} %reshape.195, bf16[8,128,1024]{2,1,0:T(8,128)(2,1)} %get-tuple-element.204), kind=kOutput, calls=%fused_computation.5.clone.1 | convolution fusion | flops 268435456 | bytes 2884608 | tf_op jit(solution)/shard_map/while/body/eval_jaxpr/xm,smz->sxz/dot_general | solution.py:90
  174.4 0.7 fusion.44
  175.2 2.1 gather_fusion
  177.6 5.2 %convolution_convert_fusion.2 = bf16[64,16384]{1,0:T(8,128)(2,1)} fusion(bf16[168,16384]{1,0:T(8,128)(2,1)} %get-tuple-element.203, s32[64]{0:T(128)S(1)} %eq.70, pred[64]{0:T(512)(128)(4,1)S(1)} %gt.17), kind=kOutput, calls=%fused_computation.3.clone.1 | convolution fusion | flops 353391616 | bytes 7602496 | tf_op jit(solution)/shard_map/while/body/eval_jaxpr/dot_general | solution.py:86
  182.8 4.2 %reshape.195 = bf16[8,1024,128]{2,1,0:T(8,128)(2,1)} reshape(bf16[64,16384]{1,0:T(8,128)(2,1)} %convolution_convert_fusion.2) | data formatting | bytes 4194304 | tf_op jit(solution)/shard_map/while/body/eval_jaxpr/reshape | solution.py:89
  187.1 3.1 %fusion.46 = f32[8,8,128,128]{2,3,0,1:T(8,128)} fusion(f32[8,8,128,128]{2,3,0,1:T(8,128)} %get-tuple-element.189, s32[]{:T(128)} %get-tuple-element.188, bf16[8,1024,128]{2,1,0:T(8,128)(2,1)} %reshape.195, bf16[8,128,1024]{2,1,0:T(8,128)(2,1)} %get-tuple-element.204), kind=kOutput, calls=%fused_computation.5.clone.1 | convolution fusion | flops 268435456 | bytes 2884608 | tf_op jit(solution)/shard_map/while/body/eval_jaxpr/xm,smz->sxz/dot_general | solution.py:90
  190.2 4.7 %all-to-all-start = ((f32[8,8,1,128,128]{3,4,1,2,0:T(8,128)}), f32[8,8,1,128,128]{3,4,1,2,0:T(8,128)}, u32[]{:S(2)}, u32[]{:S(2)}) async-start(f32[8,8,1,128,128]{3,4,1,2,0:T(8,128)} %bitcast.69), calls=%async_computation | async-start | bytes 8388608 | tf_op jit(solution)/shard_map/all_to_all | solution.py:32
  194.9 0.6 reduce_sum.46
  195.5 1.3 dynamic-slice
  196.8 1.4 dynamic-update-slice
  198.2 10.1 %all-reduce = s32[8]{0:T(128)S(1)} all-reduce(s32[8]{0:T(128)S(1)} %dynamic-update-slice), channel_id=1, replica_groups=mesh['rows_0'=8,'rows_1'=8,'inner'=8] {'rows_0'}, use_global_device_ids=true, to_apply=%add | all-reduce | flops 8 | bytes 64
  208.3 1.3 dynamic-slice.1
  210.3 0.2 dynamic-update-slice.1
  210.5 15.2 %all-reduce.1 = s32[64]{0:T(128)S(1)} all-reduce(s32[64]{0:T(128)S(1)} %dynamic-update-slice.1), channel_id=1, replica_groups=mesh['rows_0'=8,'rows_1'=8,'inner'=8] {'rows_1'}, use_global_device_ids=true, to_apply=%add.1 | all-reduce | flops 64 | bytes 512
  225.8 0.2 reduce-window.9
  226.0 0.6 fusion.24
  226.6 1.2 bitcast_subtract_fusion
  227.7 16.8 %all-to-all-done = f32[8,8,1,128,128]{3,4,1,2,0:T(8,128)} async-done(((f32[8,8,1,128,128]{3,4,1,2,0:T(8,128)}), f32[8,8,1,128,128]{3,4,1,2,0:T(8,128)}, u32[]{:S(2)}, u32[]{:S(2)}) %all-to-all-start) | async-done | bytes 4194336 | tf_op jit(solution)/shard_map/all_to_all | solution.py:32
  244.5 2.5 %reduce_sum.45 = bf16[8,128,128]{1,2,0:T(8,128)(2,1)S(1)} reduce(f32[8,8,1,128,128]{3,4,1,2,0:T(8,128)} %all-to-all-done, f32[]{:T(128)} %constant.65.clone.1), dimensions={0,2}, to_apply=%region_4.5 | reduce | flops 917504 | bytes 4456452 | tf_op jit(solution)/shard_map/reduce_sum | solution.py:33
  247.0 0.9 copy.23
  (76 shorter events, 2.9 us)
Async XLA Ops:
  0.6 16.7 %copy-start = (bf16[8,8,128,128]{3,2,1,0:T(8,128)(2,1)S(1)}, bf16[8,8,128,128]{3,2,1,0:T(8,128)(2,1)}, u32[]{:S(2)}) copy-start(bf16[8,8,128,128]{3,2,1,0:T(8,128)(2,1)} %param.8) | copy-start | bytes 6291460
  0.6 16.7 %copy-start.2 = (s32[8,8]{1,0:T(8,128)S(1)}, s32[8,8]{1,0:T(8,128)}, u32[]{:S(2)}) copy-start(s32[8,8]{1,0:T(8,128)} %param.9) | copy-start | bytes 772
  0.7 52.2 %collective-permute-start = (bf16[8,7,128,128]{3,2,1,0:T(8,128)(2,1)}, bf16[8,7,128,128]{3,2,1,0:T(8,128)(2,1)}, u32[]{:S(2)}, u32[]{:S(2)}) collective-permute-start(bf16[8,7,128,128]{3,2,1,0:T(8,128)(2,1)} %param.10), channel_id=1, source_target_pairs={{0,8},{8,16},{16,24},{24,32},{32,40},{40,48},{48,56},{56,64},{64,7... | collective-permute-start | bytes 5505032 | tf_op jit(solution)/shard_map/ppermute | solution.py:16
  5.1 48.9 %collective-permute-start.1 = (bf16[8,7,128,128]{3,2,1,0:T(8,128)(2,1)}, bf16[8,7,128,128]{3,2,1,0:T(8,128)(2,1)}, u32[]{:S(2)}, u32[]{:S(2)}) collective-permute-start(bf16[8,7,128,128]{3,2,1,0:T(8,128)(2,1)} %param.10), channel_id=1, source_target_pairs={{8,0},{16,8},{24,16},{32,24},{40,32},{48,40},{56,48},{64,56},{72,6... | collective-permute-start | bytes 5505032 | tf_op jit(solution)/shard_map/ppermute | solution.py:19
  17.4 36.6 %copy-start.1 = (bf16[8,7,128,128]{3,2,1,0:T(8,128)(2,1)S(1)}, bf16[8,7,128,128]{3,2,1,0:T(8,128)(2,1)}, u32[]{:S(2)}) copy-start(bf16[8,7,128,128]{3,2,1,0:T(8,128)(2,1)} %param.10) | copy-start | bytes 5505028
  190.2 4.7 %copy-start.3 = (s32[8]{0:T(128)S(1)}, s32[8]{0:T(128)}, u32[]{:S(2)}) copy-start(s32[8]{0:T(128)} %param.13) | copy-start | bytes 100
  190.2 54.3 %all-to-all-start = ((f32[8,8,1,128,128]{3,4,1,2,0:T(8,128)}), f32[8,8,1,128,128]{3,4,1,2,0:T(8,128)}, u32[]{:S(2)}, u32[]{:S(2)}) async-start(f32[8,8,1,128,128]{3,4,1,2,0:T(8,128)} %bitcast.69), calls=%async_computation | async-start | bytes 8388608 | tf_op jit(solution)/shard_map/all_to_all | solution.py:32
where the time goes:
time: 250 us; the launch traced here: 248 us
  local copies, waits for them, and re-layouts  70.2 us (28%)
  matrix products  66.6 us (27%)
  waiting for transfers between devices  51.6 us (21%)
  blocking collectives  25.3 us (10%)
  starting transfers between devices  18.5 us (7%)
  other arithmetic  14.2 us (6%)
    dot_general x8, matrix products, row_partial(): jnp.dot(selector, flat_tiles, preferred_element_type=jnp.float32)  41.4 us
    reshape x8, local copies, waits for them, and re-layouts, row_partial(): chosen = chosen.reshape(wanted.shape[0], r_slots * tile_size, tile_size)  33.9 us
    ppermute x1, waiting for transfers between devices, padded(): lax.ppermute(lax.slice_in_dim(block, block.shape[dim] - width, None, axis...  33.7 us
    unnamed x2, blocking collectives  25.3 us
    dot_general x8, matrix products, row_partial(): jnp.einsum('xm,smz->sxz', row_wide, chosen, preferred_element_type=jnp.fl...  25.2 us
    gather x16, local copies, waits for them, and re-layouts, row_partial(): matches = wanted[:, None, None] == a_cols[columns][None]  17.8 us
    all_to_all x1, waiting for transfers between devices, sent_and_summed(): parts = lax.all_to_all(split_up(value, dim, size), axis, 0, 0, tiled=True)  16.8 us
    unnamed x17, local copies, waits for them, and re-layouts  15.3 us
  transfers between devices with their start and end apart: 3, of which 3 were waited for; matrix products, arithmetic and copies ran while one was open for 5% of the time, Pallas kernels for 0%

commit v1 on v0

v1 whole, which is shorter than its diff:
```python
import functools

import jax
import jax.numpy as jnp
from jax import lax
from jax.experimental import pallas as pl
from jax.experimental.pallas import tpu as pltpu
from jax.sharding import Mesh
from jax.sharding import PartitionSpec as P

I32 = jnp.int32
F32 = jnp.float32
BF16 = jnp.bfloat16
ROWS = ("r0", "r1")
INNER = ("x", "core")
EVERY = ROWS + INNER
FIRST = ("r0", "core")
SECOND = ("r1", "x")
LANES = 128
PACK = 20
STEPS = 256.0
TOP = 32766.0
UNROLL = 4
HEAD = 8


def slot_words(r_ref, c_ref, kinds, keys, count):
    for c in range(count):
        used = jnp.zeros_like(keys)
        fed = jnp.zeros_like(keys)
        for n in range(count):
            used = jnp.where(keys == r_ref[c, n], n + 1, used)
            fed = jnp.where(kinds == c_ref[c, n], n + 1, fed)
        yield c, used, fed


def plan_kernel(wants_ref, win_ref, list_ref, words, table, sem, *, fine, groups, blocks):
    slots = win_ref.shape[1]
    rows = wants_ref.shape[1]
    row = lax.axis_index(ROWS)
    group = lax.axis_index(INNER)
    lane = lax.broadcasted_iota(I32, (slots, LANES), 1)
    half = rows // 2
    for src in range(3):
        first = (row - 1 + src) * (groups * fine) + group * fine
        block = jnp.clip(lax.div(first + LANES, LANES) - 1, 0, blocks - 1)
        keys = block * LANES + lane
        own = (keys >= first) & (keys < first + fine)
        packed = [jnp.zeros((slots, LANES), I32), jnp.zeros((slots, LANES), I32)]
        for c, used, fed in slot_words(wants_ref.at[0], wants_ref.at[1], win_ref[src], keys, rows):
            code = jnp.where(own & (used > 0) & (fed > 0), (fed - 1) * rows + used, 0)
            packed[c // half] = packed[c // half] | (code << (7 * (c % half)))
        words[src, 0, :slots] = packed[0]
        words[src, 1, :slots] = packed[1]
        slot = lax.broadcasted_iota(I32, (slots, LANES), 0)
        marks = jnp.where((packed[0] | packed[1]) != 0, jnp.left_shift(1, slot), 0)
        words[src, 0, slots : slots + 1] = jnp.sum(marks, axis=0, keepdims=True)
    copy = pltpu.make_async_copy(words, table, sem)
    copy.start()
    copy.wait()

    n = jnp.int32(HEAD)
    for src in range(3):
        first = (row - 1 + src) * (groups * fine) + group * fine
        base = lax.rem(first + LANES, LANES)
        began = n

        def fine_row(q, carry, src=src, base=base):
            n, place = carry
            mark = table[src, 0, slots, base + q]

            def found(n, place):
                for t in range(slots):

                    def pairs(n, place, t=t):
                        spot = q * slots + t if src == 1 else place
                        low = table[src, 0, t, base + q]
                        high = table[src, 1, t, base + q]
                        for c in range(rows):
                            code = ((low if c < half else high) >> (7 * (c % half))) & 127
                            list_ref[n] = spot * 512 + c * 64 + jnp.maximum(code - 1, 0)
                            n = n + (code > 0).astype(I32)
                        return n, place + 1

                    n, place = lax.cond((mark & (1 << t)) != 0, pairs, lambda n, place: (n, place), n, place)
                return n, place

            return lax.cond(mark != 0, found, lambda n, place: (n, place), n, place)

        n, _ = lax.fori_loop(0, fine, fine_row, (n, jnp.int32(0)))
        list_ref[src] = n - began


def pack_kernel(
    round_ref, up_ref, down_ref, counts_ref, win_ref, a_ref, up_out, down_out, told_ref, need, flags, sem, copy_sem, *, fine, groups, blocks
):
    slots = win_ref.shape[0]
    rows = up_ref.shape[1]
    pack = up_out.shape[0]
    row = lax.axis_index(ROWS)
    group = lax.axis_index(INNER)
    first = row * (groups * fine) + group * fine
    base = lax.rem(first, LANES)
    lane = lax.broadcasted_iota(I32, (slots, LANES), 1)
    keys = first - base + lane
    own = (keys >= first) & (keys < first + fine)
    for side, ref in enumerate((up_ref, down_ref)):
        wanted = jnp.zeros((slots, LANES), I32)
        for _, used, fed in slot_words(ref.at[0], ref.at[1], win_ref[...], keys, rows):
            wanted = jnp.where(own & (used > 0) & (fed > 0), 1, wanted)
        need[side, :slots] = wanted
    copy = pltpu.make_async_copy(need, flags, sem)
    copy.start()
    copy.wait()
    start = round_ref[0] * pack
    outs = (up_out, down_out)

    def fine_row(q, carry):
        places = list(carry)
        for t in range(slots):
            for side in range(2):
                flag = flags[side, t, base + q]
                place = places[side] - start

                @pl.when((flag > 0) & (place >= 0) & (place < pack))
                def _(side=side, t=t, place=place):
                    pltpu.make_async_copy(a_ref.at[q, t], outs[side].at[place], copy_sem).start()

                places[side] = places[side] + flag
        return tuple(places)

    up_count, down_count = lax.fori_loop(0, fine, fine_row, (jnp.int32(0), jnp.int32(0)))
    sent = jnp.clip(up_count - start, 0, pack) + jnp.clip(down_count - start, 0, pack)

    @pl.loop(0, sent)
    def _(i):
        pltpu.make_async_copy(a_ref.at[0, 0], up_out.at[0], copy_sem).wait()

    total = counts_ref[0]
    for c in range(1, rows):
        total = total + counts_ref[c]
    lane = lax.broadcasted_iota(I32, (1, LANES), 1)
    mine = jnp.where((lane == row) & (group == 0), total, 0)
    over = jnp.maximum(up_count, down_count) > (lane - (blocks - 1)) * pack
    words = mine + jnp.where((lane >= blocks) & over, 1, 0)
    for i in range(told_ref.shape[0]):
        told_ref[i] = words


def product_kernel(round_ref, list_ref, r_ref, own_ref, low_ref, high_ref, *rest, fresh):
    keep_ref, send_ref = rest[-2:]
    pack = low_ref.shape[0]
    cells = keep_ref.shape[0] - 1
    rows = r_ref.shape[0]
    core = lax.axis_index("core")

    @pl.loop(0, cells)
    def _(i):
        for out, old in zip(rest[-2:], rest[:-2] if not fresh else (None, None)):
            out[i] = jnp.zeros(out.shape[1:], F32) if fresh else old[i]

    start = round_ref[0] * pack
    begin = jnp.int32(HEAD)
    for src, ref in enumerate((low_ref, own_ref, high_ref)):
        end = begin + list_ref[src]
        if src == 1 and not fresh:
            begin = end
            continue

        @pl.loop(0, lax.div(end - begin + UNROLL - 1, UNROLL))
        def _(i, src=src, ref=ref, begin=begin, end=end):
            for u in range(UNROLL):
                at = begin + i * UNROLL + u
                entry = list_ref[at]
                place = lax.shift_right_logical(entry, 9)
                row = lax.shift_right_logical(entry, 6) & 7
                slot = lax.shift_right_logical(entry, 3) & 7
                live = at < end
                if src != 1:
                    place = place - start
                    live = live & (place >= 0) & (place < pack)
                place = jnp.where(live, place, 0)
                cell = lax.shift_right_logical(slot, 1) * rows + (row & 7)
                kept = (slot & 1) == core
                part = jnp.dot(r_ref[row & 7, entry & 7], ref[place], preferred_element_type=F32)
                mine = jnp.where(live & kept, cell, cells)
                theirs = jnp.where(live & jnp.logical_not(kept), cell, cells)
                keep_ref[mine] = keep_ref[mine] + part
                send_ref[theirs] = send_ref[theirs] + part

        begin = end


def code_kernel(x_ref, keep_ref, got_ref, own_out, *outs):
    rows, size = own_out.shape[:2]
    step = pl.program_id(0)

    @pl.when(step == len(outs))
    def _():
        own_out[...] = keep_ref[...] + got_ref[...]

    for d, out in enumerate(outs):

        @pl.when(step == d)
        def _(out=out):
            levels = []
            for c in range(rows):
                value = keep_ref[c] + got_ref[c]
                top = jnp.max(jnp.abs(value), axis=0, keepdims=True)
                level = jnp.ceil(jnp.log2(jnp.maximum(top, 1e-30)) * STEPS) + 1.0
                code = jnp.round(value * (jnp.exp2(level * (-1.0 / STEPS)) * TOP))
                out[pl.ds(c * size, size)] = code.astype(I32).astype(jnp.int16)
                levels.append(level)
            levels = jnp.concatenate(levels + levels, axis=0)
            out[pl.ds(rows * size, 2 * rows)] = levels.astype(I32).astype(jnp.int16)


def decode_kernel(own_ref, *refs):
    parts, out_ref = refs[:-1], refs[-1]
    rows = out_ref.shape[0]
    size = out_ref.shape[2]
    scales = [jnp.exp2(p[pl.ds(rows * size, 2 * rows)].astype(F32) * (1.0 / STEPS)) * (1.0 / TOP) for p in parts]
    for c in range(rows):
        total = own_ref[c]
        for p, scale in zip(parts, scales):
            total = total + p[pl.ds(c * size, size)].astype(F32) * scale[c : c + 1]
        out_ref[c, 0] = total.astype(BF16)


def offset_kernel(counts_ref, parts_ref, out_ref, turns_ref, *, blocks):
    row = lax.axis_index(ROWS)
    words = parts_ref[0]
    for i in range(1, parts_ref.shape[0]):
        words = words + parts_ref[i]
    lane = lax.broadcasted_iota(I32, words.shape, 1)
    turns_ref[0] = 1 + jnp.sum(((lane >= blocks) & (words > 0)).astype(I32))
    offset = jnp.sum(jnp.where(lane < row, words, 0))
    for c in range(out_ref.shape[0]):
        out_ref[c] = offset
        offset = offset + counts_ref[c]


def smem():
    return pl.BlockSpec(memory_space=pltpu.SMEM)


def vmem():
    return pl.BlockSpec(memory_space=pltpu.VMEM)


def anywhere():
    return pl.BlockSpec(memory_space=pl.ANY)


def shape(dims, dtype):
    return jax.ShapeDtypeStruct(dims, dtype)


def told(parts, axes):
    return jnp.sum(lax.all_to_all(parts, axes, 0, 0, tiled=True), axis=(0, 1))


def body(r_tiles, r_cols, a_tiles, a_cols, c_cols, c_counts):
    fine, op_slots, size, _ = a_tiles.shape
    rows, r_slots = r_tiles.shape[:2]
    groups = lax.axis_size(INNER)
    chips = lax.axis_size("x")
    row_blocks = lax.axis_size(ROWS)
    row = lax.axis_index(ROWS)
    group = lax.axis_index(INNER)
    blocks = a_cols.shape[0] // LANES
    pack = PACK
    cap = c_cols.shape[1]
    limit = lambda mb: pltpu.CompilerParams(vmem_limit_bytes=mb * 2**20)

    to_next = [(i, i + 1) for i in range(row_blocks - 1)]
    to_last = [(i + 1, i) for i in range(row_blocks - 1)]

    wants = jnp.stack([r_cols, c_cols])
    above = lax.ppermute(wants, ROWS, to_last)
    below = lax.ppermute(wants, ROWS, to_next)

    by_slot = a_cols.T

    def window(block_row):
        first = block_row * (groups * fine) + group * fine
        block = jnp.clip((first + LANES) // LANES - 1, 0, blocks - 1)
        return lax.dynamic_slice(by_slot, (0, block * LANES), (op_slots, LANES))

    own_window = window(row)
    windows = jnp.stack([window(row - 1), own_window, window(row + 1)])
    pairs = pl.pallas_call(
        functools.partial(plan_kernel, fine=fine, groups=groups, blocks=blocks),
        in_specs=[smem(), vmem()],
        out_specs=smem(),
        out_shape=shape((rows * r_slots * op_slots + 64,), I32),
        scratch_shapes=[
            pltpu.VMEM((3, 2, 8, LANES), I32),
            pltpu.SMEM((3, 2, 8, LANES), I32),
            pltpu.SemaphoreType.DMA,
        ],
        compiler_params=limit(4),
        name="plan",
    )(wants, windows)

    own_tiles = a_tiles.reshape(fine * op_slots, size, size)

    firsts, seconds = lax.axis_size(FIRST), lax.axis_size(SECOND)

    def exchange(turn):
        up, down, words = pl.pallas_call(
            functools.partial(pack_kernel, fine=fine, groups=groups, blocks=row_blocks),
            in_specs=[smem(), smem(), smem(), smem(), vmem(), anywhere()],
            out_specs=[anywhere(), anywhere(), vmem()],
            out_shape=[
                shape((pack, size, size), BF16),
                shape((pack, size, size), BF16),
                shape((firsts, 1, LANES), I32),
            ],
            scratch_shapes=[
                pltpu.VMEM((2, 8, LANES), I32),
                pltpu.SMEM((2, 8, LANES), I32),
                pltpu.SemaphoreType.DMA,
                pltpu.SemaphoreType.DMA,
            ],
            compiler_params=limit(4),
            name="pack",
        )(turn, above, below, c_counts, own_window, a_tiles)
        low = lax.ppermute(up, ROWS, to_next)
        high = lax.ppermute(down, ROWS, to_last)
        return low, high, words

    half = (chips * rows + 1, size, size)

    def product(turn, low, high, sums):
        fresh = sums is None
        return pl.pallas_call(
            functools.partial(product_kernel, fresh=fresh),
            in_specs=[smem(), smem()] + [vmem()] * (4 if fresh else 6),
            out_specs=[vmem(), vmem()],
            out_shape=[shape(half, F32)] * 2,
            compiler_params=limit(20),
            name="products" if fresh else "more_products",
        )(turn, pairs, r_tiles, own_tiles, low, high, *(() if fresh else sums))

    coded_rows = rows * size + 2 * rows
    chip = lax.axis_index("x")[None]
    others = range(1, chips)

    def chunk(i, x):
        return (lax.rem(x[0] + i + 1, chips), 0, 0)

    def coded(keep, send):
        got = lax.ppermute(send, "core", [(0, 1), (1, 0)])
        return pl.pallas_call(
            code_kernel,
            grid_spec=pltpu.PrefetchScalarGridSpec(
                num_scalar_prefetch=1,
                grid=(chips,),
                in_specs=[pl.BlockSpec((rows, size, size), chunk)] * 2,
                out_specs=[pl.BlockSpec((rows, size, size), lambda i, x: (0, 0, 0))]
                + [pl.BlockSpec((coded_rows, size), lambda i, x: (0, 0))] * len(others),
            ),
            out_shape=[shape((rows, size, size), F32)] + [shape((coded_rows, size), jnp.int16)] * len(others),
            compiler_params=limit(20),
            name="code",
        )(chip, keep, got)

    def swapped(codes):
        return [lax.ppermute(code, "x", [(i, (i + d) % chips) for i in range(chips)]) for d, code in zip(others, codes)]

    def finish(own, parts):
        return pl.pallas_call(
            decode_kernel,
            in_specs=[vmem()] * chips,
            out_specs=vmem(),
            out_shape=shape((rows, 1, size, size), BF16),
            compiler_params=limit(16),
            name="decode",
        )(own, *parts)

    low, high, words = exchange(jnp.zeros((1,), I32))
    shared = told(words, FIRST)
    turn, shared = lax.optimization_barrier((jnp.zeros((1,), I32), shared))
    keep, send = product(turn, low, high, None)
    own, *codes = coded(keep, send)
    parts = swapped(codes)
    shared = jnp.broadcast_to(shared[None, None], (seconds, 1, LANES))
    shared = lax.all_to_all(shared, SECOND, 0, 0, tiled=True)
    c_tiles = finish(own, parts)
    row_offsets, turns = pl.pallas_call(
        functools.partial(offset_kernel, blocks=row_blocks),
        in_specs=[smem(), vmem()],
        out_specs=[smem(), smem()],
        out_shape=[shape((rows,), I32), shape((1,), I32)],
        compiler_params=limit(4),
        name="offsets",
    )(c_counts, shared)

    def more(state):
        turn, keep, send, _ = state
        low, high, _ = exchange(turn[None])
        keep, send = product(turn[None], low, high, (keep, send))
        own, *codes = coded(keep, send)
        return turn + 1, keep, send, finish(own, swapped(codes))

    state = (jnp.int32(1), keep, send, c_tiles)
    c_tiles = lax.while_loop(lambda state: state[0] < turns[0], more, state)[3]
    return (c_tiles, row_offsets)


def solution(mesh):
    finer = Mesh(mesh.devices.reshape(8, mesh.shape["rows"] // 8, mesh.shape["inner"] // 2, 2), EVERY)
    return jax.shard_map(
        body,
        mesh=finer,
        in_specs=(
            P(ROWS, INNER, None, None),
            P(ROWS, INNER),
            P(EVERY, None, None, None),
            P(),
            P(ROWS, None),
            P(ROWS),
        ),
        out_specs=(P(ROWS, INNER, None, None), P(ROWS)),
        check_vma=False,
    )
```

time: 250 us -> 90.7 us (0.36)
  the two profiles are of different devices: /device:TPU:40 before, /device:TPU:8 now
where the time goes in v1:
time: 90.7 us; the launch traced here: 89.9 us
  starting transfers between devices  47.6 us (52%)
  waiting for transfers between devices  23.8 us (26%)
  Pallas kernels  14.9 us (16%)
  local copies, waits for them, and re-layouts  1.4 us (2%)
    ppermute x3, starting transfers between devices, swapped(): lax.ppermute(code, 'x', [(i, (i + d) % chips) for i in range(chips)])  11.2 us
    ppermute x1, starting transfers between devices, body(): above = lax.ppermute(wants, ROWS, to_last)  10.8 us
    all_to_all x1, starting transfers between devices, told(): return jnp.sum(lax.all_to_all(parts, axes, 0, 0, tiled=True), axis=(0, 1))  9.86 us
    all_to_all x1, waiting for transfers between devices, body(): shared = lax.all_to_all(shared, SECOND, 0, 0, tiled=True)  9.69 us
    ppermute x1, starting transfers between devices, exchange(): high = lax.ppermute(down, ROWS, to_last)  6.03 us
    pallas_call x1, Pallas kernels, body(): pl.pallas_call(functools.partial(plan_kernel, fine=fine, groups=groups, b...  5.19 us
    all_to_all x1, waiting for transfers between devices, told(): return jnp.sum(lax.all_to_all(parts, axes, 0, 0, tiled=True), axis=(0, 1))  5 us
    ppermute x1, waiting for transfers between devices, body(): below = lax.ppermute(wants, ROWS, to_next)  4.89 us
  transfers between devices with their start and end apart: 10, of which 4 were waited for; matrix products, arithmetic and copies ran while one was open for 2% of the time, Pallas kernels for 7%

profile of v1, /device:TPU:8, one launch (start us, length us, event | category | flops | bytes accessed | tf_op | source)
XLA Modules:
  0.0 89.9 jit_solution(13838142067370870341)
XLA Ops:
  0.6 0.7 pad_add_fusion.1.wants_ref
  1.3 10.8 %collective-permute-start.6 = (s32[2,8,8]{2,1,0:T(8,128)S(1)}, s32[2,8,8]{2,1,0:T(8,128)S(1)}, u32[]{:S(2)}, u32[]{:S(2)}) collective-permute-start(s32[2,8,8]{2,1,0:T(8,128)S(1)} %pad_add_fusion.1.wants_ref), channel_id=1, source_target_pairs={{8,0},{16,8},{24,16},{32,24},{40,32},{48,40},{56,48},{64,56},{72,6... | collective-permute-start | bytes 1544 | tf_op jit(solution)/shard_map/ppermute | solution.py:280
  12.2 1.9 %collective-permute-start.7 = (s32[2,8,8]{2,1,0:T(8,128)S(1)}, s32[2,8,8]{2,1,0:T(8,128)S(1)}, u32[]{:S(2)}, u32[]{:S(2)}) collective-permute-start(s32[2,8,8]{2,1,0:T(8,128)S(1)} %pad_add_fusion.1.wants_ref), channel_id=1, source_target_pairs={{0,8},{8,16},{16,24},{24,32},{32,40},{40,48},{48,56},{56,64},{64,7... | collective-permute-start | bytes 1544 | tf_op jit(solution)/shard_map/ppermute | solution.py:281
  14.2 0.8 dynamic-slice_bitcast_fusion.1
  14.9 0.0 collective-permute-done.6.up_ref
  14.9 4.9 %collective-permute-done.7.down_ref = s32[2,8,8]{2,1,0:T(8,128)S(1)} collective-permute-done((s32[2,8,8]{2,1,0:T(8,128)S(1)}, s32[2,8,8]{2,1,0:T(8,128)S(1)}, u32[]{:S(2)}, u32[]{:S(2)}) %collective-permute-start.7) | collective-permute-done | bytes 544 | tf_op jit(solution)/shard_map/ppermute | solution.py:281
  19.8 3.7 %pack.2 = (bf16[20,128,128]{2,1,0:T(8,128)(2,1)S(1)}, bf16[20,128,128]{2,1,0:T(8,128)(2,1)S(1)}, s32[16,1,128]{2,1,0:T(1,128)}) custom-call(s32[1]{0:T(128)} %constant.52.clone.1.round_ref, s32[2,8,8]{2,1,0:T(8,128)S(1)} %collective-permute-done.6.up_ref, s32[2,8,8]{2,1,0:T(8,128)S(1)} %collective-permute-done.7.down_ref, s32[8]{0:T(128)} %counts_ref.3, ...), custom_call_target="tpu_custom_call" | custom-call | tf_op jit(solution)/shard_map/pack/pallas_call | solution.py:311
  23.5 1.9 %collective-permute-start.8 = (bf16[20,128,128]{2,1,0:T(8,128)(2,1)S(1)}, bf16[20,128,128]{2,1,0:T(8,128)(2,1)S(1)}, u32[]{:S(2)}, u32[]{:S(2)}) collective-permute-start(bf16[20,128,128]{2,1,0:T(8,128)(2,1)S(1)} %get-tuple-element.97), channel_id=1, source_target_pairs={{0,8},{8,16},{16,24},{24,32},{32,40},{40,48},{48,56},{56,64},{64,7... | collective-permute-start | bytes 1966088 | tf_op jit(solution)/shard_map/ppermute | solution.py:329
  25.5 6.0 %collective-permute-start.9 = (bf16[20,128,128]{2,1,0:T(8,128)(2,1)S(1)}, bf16[20,128,128]{2,1,0:T(8,128)(2,1)S(1)}, u32[]{:S(2)}, u32[]{:S(2)}) collective-permute-start(bf16[20,128,128]{2,1,0:T(8,128)(2,1)S(1)} %get-tuple-element.98), channel_id=1, source_target_pairs={{8,0},{16,8},{24,16},{32,24},{40,32},{48,40},{56,48},{64,56},{72,6... | collective-permute-start | bytes 1966088 | tf_op jit(solution)/shard_map/ppermute | solution.py:330
  31.5 9.9 %all-to-all-start = ((s32[16,1,128]{2,1,0:T(1,128)}), s32[16,1,128]{2,1,0:T(1,128)S(1)}, u32[]{:S(2)}, u32[]{:S(2)}) async-start(s32[16,1,128]{2,1,0:T(1,128)} %get-tuple-element.95), calls=%async_computation | async-start | bytes 16384 | tf_op jit(solution)/shard_map/all_to_all | solution.py:260
  41.4 5.2 %plan.1.list_ref = s32[512]{0:T(512)S(1)} custom-call(s32[2,8,8]{2,1,0:T(8,128)S(1)} %pad_add_fusion.1.wants_ref, s32[3,7,128]{2,1,0:T(8,128)S(1)} %pad_add_fusion.win_ref), custom_call_target="tpu_custom_call" | custom-call | tf_op jit(solution)/shard_map/plan/pallas_call | solution.py:292
  46.6 5.0 %all-to-all-done = s32[16,1,128]{2,1,0:T(1,128)S(1)} async-done(((s32[16,1,128]{2,1,0:T(1,128)}), s32[16,1,128]{2,1,0:T(1,128)S(1)}, u32[]{:S(2)}, u32[]{:S(2)}) %all-to-all-start) | async-done | bytes 8224 | tf_op jit(solution)/shard_map/all_to_all | solution.py:260
  51.6 0.0 collective-permute-done.8.low_ref
  51.6 0.0 collective-permute-done.9.high_ref
  51.6 3.3 %products.1 = (f32[33,128,128]{2,1,0:T(8,128)S(1)}, f32[33,128,128]{2,1,0:T(8,128)S(1)}) custom-call(s32[1]{0:T(128)} %constant.52.clone.1.round_ref, s32[512]{0:T(512)S(1)} %plan.1.list_ref, bf16[8,8,128,128]{3,2,1,0:T(8,128)(2,1)} %r_ref.1, bf16[56,128,128]{2,1,0:T(8,128)(2,1)} %bitcast.22, bf16[20,128,128]{2,1,0:T(8,128)(2,1)S(1)} %collective-permute-done.8.low_ref, ...), custom_call_target="tpu_custom_call" | custom-call | tf_op jit(solution)/shard_map/products/pallas_call | solution.py:337
  54.9 0.0 copy-start.1
  54.9 0.0 copy-start.4
  54.9 1.9 %collective-permute-start.10 = (f32[33,128,128]{2,1,0:T(8,128)S(1)}, f32[33,128,128]{2,1,0:T(8,128)S(1)}, u32[]{:S(2)}, u32[]{:S(2)}) collective-permute-start(f32[33,128,128]{2,1,0:T(8,128)S(1)} %get-tuple-element.243), channel_id=1, source_target_pairs={{0,1},{1,0},{2,3},{3,2},{4,5},{5,4},{6,7},{7,6},{8,9},{9,8},{10,11... | collective-permute-start | bytes 6488072 | tf_op jit(solution)/shard_map/ppermute | solution.py:354
  56.9 4.2 %collective-permute-done.10.got_ref = f32[33,128,128]{2,1,0:T(8,128)S(1)} collective-permute-done((f32[33,128,128]{2,1,0:T(8,128)S(1)}, f32[33,128,128]{2,1,0:T(8,128)S(1)}, u32[]{:S(2)}, u32[]{:S(2)}) %collective-permute-start.10) | collective-permute-done | bytes 2162720 | tf_op jit(solution)/shard_map/ppermute | solution.py:354
  61.1 0.0 copy-start.6
  61.1 0.6 code.2
  61.7 0.0 copy-done.1
  61.7 0.0 copy-done.4
  61.7 3.4 %collective-permute-start.11 = (s16[1040,128]{1,0:T(8,128)(2,1)S(1)}, s16[1040,128]{1,0:T(8,128)(2,1)S(1)}, u32[]{:S(2)}, u32[]{:S(2)}) collective-permute-start(s16[1040,128]{1,0:T(8,128)(2,1)S(1)} %get-tuple-element.102), channel_id=1, source_target_pairs={{0,2},{2,4},{4,6},{6,0},{1,3},{3,5},{5,7},{7,1},{8,10},{10,12},{12... | collective-permute-start | bytes 798728 | tf_op jit(solution)/shard_map/ppermute | solution.py:370
  65.0 4.9 %collective-permute-start.12 = (s16[1040,128]{1,0:T(8,128)(2,1)S(1)}, s16[1040,128]{1,0:T(8,128)(2,1)S(1)}, u32[]{:S(2)}, u32[]{:S(2)}) collective-permute-start(s16[1040,128]{1,0:T(8,128)(2,1)S(1)} %get-tuple-element.103), channel_id=1, source_target_pairs={{0,4},{2,6},{4,0},{6,2},{1,5},{3,7},{5,1},{7,3},{8,12},{10,14},{12... | collective-permute-start | bytes 798728 | tf_op jit(solution)/shard_map/ppermute | solution.py:370
  69.9 3.0 %collective-permute-start.13 = (s16[1040,128]{1,0:T(8,128)(2,1)S(1)}, s16[1040,128]{1,0:T(8,128)(2,1)S(1)}, u32[]{:S(2)}, u32[]{:S(2)}) collective-permute-start(s16[1040,128]{1,0:T(8,128)(2,1)S(1)} %get-tuple-element.104), channel_id=1, source_target_pairs={{0,6},{2,0},{4,2},{6,4},{1,7},{3,1},{5,3},{7,5},{8,14},{10,8},{12,... | collective-permute-start | bytes 798728 | tf_op jit(solution)/shard_map/ppermute | solution.py:370
  72.9 0.6 broadcast_in_dim.14
  73.5 3.8 %all-to-all-start.1 = ((s32[32,1,128]{2,1,0:T(1,128)}), s32[32,1,128]{2,1,0:T(1,128)S(1)}, u32[]{:S(2)}, u32[]{:S(2)}) async-start(s32[32,1,128]{2,1,0:T(1,128)} %broadcast_in_dim.14), calls=%async_computation.1 | async-start | bytes 32768 | tf_op jit(solution)/shard_map/all_to_all | solution.py:389
  77.4 9.7 %all-to-all-done.1.parts_ref = s32[32,1,128]{2,1,0:T(1,128)S(1)} async-done(((s32[32,1,128]{2,1,0:T(1,128)}), s32[32,1,128]{2,1,0:T(1,128)S(1)}, u32[]{:S(2)}, u32[]{:S(2)}) %all-to-all-start.1) | async-done | bytes 16416 | tf_op jit(solution)/shard_map/all_to_all | solution.py:389
  87.1 0.0 copy-done.6
  87.1 1.2 %offsets.1 = (s32[8]{0:T(128)}, s32[1]{0:T(128)}) custom-call(s32[8]{0:T(128)S(1)} %copy-done.6, s32[32,1,128]{2,1,0:T(1,128)S(1)} %all-to-all-done.1.parts_ref), custom_call_target="tpu_custom_call" | custom-call | tf_op jit(solution)/shard_map/offsets/pallas_call | solution.py:391
  88.3 0.0 collective-permute-done.11.refs_0_
  88.3 0.0 collective-permute-done.12.refs_1_
  88.3 0.0 collective-permute-done.13.refs_2_
  88.3 0.9 %decode.2 = bf16[8,1,128,128]{3,2,1,0:T(8,128)(2,1)} custom-call(f32[8,128,128]{2,1,0:T(8,128)S(1)} %get-tuple-element.101.own_ref, s16[1040,128]{1,0:T(8,128)(2,1)S(1)} %collective-permute-done.11.refs_0_, s16[1040,128]{1,0:T(8,128)(2,1)S(1)} %collective-permute-done.12.refs_1_, s16[1040,128]{1,0:T(8,128)(2,1)S(1)} %collective-permute-done.13.refs_2_), custom_call_target="tpu_custom_call" | custom-call | tf_op jit(solution)/shard_map/decode/pallas_call | solution.py:373
  89.3 0.6 while.14
  (2 shorter events, 0.0 us)
Async XLA Ops:
  1.3 13.6 %collective-permute-start.6 = (s32[2,8,8]{2,1,0:T(8,128)S(1)}, s32[2,8,8]{2,1,0:T(8,128)S(1)}, u32[]{:S(2)}, u32[]{:S(2)}) collective-permute-start(s32[2,8,8]{2,1,0:T(8,128)S(1)} %pad_add_fusion.1.wants_ref), channel_id=1, source_target_pairs={{8,0},{16,8},{24,16},{32,24},{40,32},{48,40},{56,48},{64,56},{72,6... | collective-permute-start | bytes 1544 | tf_op jit(solution)/shard_map/ppermute | solution.py:280
  12.2 7.7 %collective-permute-start.7 = (s32[2,8,8]{2,1,0:T(8,128)S(1)}, s32[2,8,8]{2,1,0:T(8,128)S(1)}, u32[]{:S(2)}, u32[]{:S(2)}) collective-permute-start(s32[2,8,8]{2,1,0:T(8,128)S(1)} %pad_add_fusion.1.wants_ref), channel_id=1, source_target_pairs={{0,8},{8,16},{16,24},{24,32},{32,40},{40,48},{48,56},{56,64},{64,7... | collective-permute-start | bytes 1544 | tf_op jit(solution)/shard_map/ppermute | solution.py:281
  23.5 28.1 %collective-permute-start.8 = (bf16[20,128,128]{2,1,0:T(8,128)(2,1)S(1)}, bf16[20,128,128]{2,1,0:T(8,128)(2,1)S(1)}, u32[]{:S(2)}, u32[]{:S(2)}) collective-permute-start(bf16[20,128,128]{2,1,0:T(8,128)(2,1)S(1)} %get-tuple-element.97), channel_id=1, source_target_pairs={{0,8},{8,16},{16,24},{24,32},{32,40},{40,48},{48,56},{56,64},{64,7... | collective-permute-start | bytes 1966088 | tf_op jit(solution)/shard_map/ppermute | solution.py:329
  25.5 26.2 %collective-permute-start.9 = (bf16[20,128,128]{2,1,0:T(8,128)(2,1)S(1)}, bf16[20,128,128]{2,1,0:T(8,128)(2,1)S(1)}, u32[]{:S(2)}, u32[]{:S(2)}) collective-permute-start(bf16[20,128,128]{2,1,0:T(8,128)(2,1)S(1)} %get-tuple-element.98), channel_id=1, source_target_pairs={{8,0},{16,8},{24,16},{32,24},{40,32},{48,40},{56,48},{64,56},{72,6... | collective-permute-start | bytes 1966088 | tf_op jit(solution)/shard_map/ppermute | solution.py:330
  31.5 20.1 %all-to-all-start = ((s32[16,1,128]{2,1,0:T(1,128)}), s32[16,1,128]{2,1,0:T(1,128)S(1)}, u32[]{:S(2)}, u32[]{:S(2)}) async-start(s32[16,1,128]{2,1,0:T(1,128)} %get-tuple-element.95), calls=%async_computation | async-start | bytes 16384 | tf_op jit(solution)/shard_map/all_to_all | solution.py:260
  54.9 6.7 %copy-start.1 = (f32[33,128,128]{2,1,0:T(8,128)}, f32[33,128,128]{2,1,0:T(8,128)S(1)}, u32[]{:S(2)}) copy-start(f32[33,128,128]{2,1,0:T(8,128)S(1)} %get-tuple-element.242.keep_ref) | copy-start | bytes 6488068
  54.9 6.7 %copy-start.4 = (f32[33,128,128]{2,1,0:T(8,128)}, f32[33,128,128]{2,1,0:T(8,128)S(1)}, u32[]{:S(2)}) copy-start(f32[33,128,128]{2,1,0:T(8,128)S(1)} %get-tuple-element.243) | copy-start | bytes 6488068
  54.9 6.1 %collective-permute-start.10 = (f32[33,128,128]{2,1,0:T(8,128)S(1)}, f32[33,128,128]{2,1,0:T(8,128)S(1)}, u32[]{:S(2)}, u32[]{:S(2)}) collective-permute-start(f32[33,128,128]{2,1,0:T(8,128)S(1)} %get-tuple-element.243), channel_id=1, source_target_pairs={{0,1},{1,0},{2,3},{3,2},{4,5},{5,4},{6,7},{7,6},{8,9},{9,8},{10,11... | collective-permute-start | bytes 6488072 | tf_op jit(solution)/shard_map/ppermute | solution.py:354
  61.1 26.0 %copy-start.6 = (s32[8]{0:T(128)S(1)}, s32[8]{0:T(128)}, u32[]{:S(2)}) copy-start(s32[8]{0:T(128)} %counts_ref.3) | copy-start | bytes 100
  61.7 26.6 %collective-permute-start.11 = (s16[1040,128]{1,0:T(8,128)(2,1)S(1)}, s16[1040,128]{1,0:T(8,128)(2,1)S(1)}, u32[]{:S(2)}, u32[]{:S(2)}) collective-permute-start(s16[1040,128]{1,0:T(8,128)(2,1)S(1)} %get-tuple-element.102), channel_id=1, source_target_pairs={{0,2},{2,4},{4,6},{6,0},{1,3},{3,5},{5,7},{7,1},{8,10},{10,12},{12... | collective-permute-start | bytes 798728 | tf_op jit(solution)/shard_map/ppermute | solution.py:370
  65.0 23.3 %collective-permute-start.12 = (s16[1040,128]{1,0:T(8,128)(2,1)S(1)}, s16[1040,128]{1,0:T(8,128)(2,1)S(1)}, u32[]{:S(2)}, u32[]{:S(2)}) collective-permute-start(s16[1040,128]{1,0:T(8,128)(2,1)S(1)} %get-tuple-element.103), channel_id=1, source_target_pairs={{0,4},{2,6},{4,0},{6,2},{1,5},{3,7},{5,1},{7,3},{8,12},{10,14},{12... | collective-permute-start | bytes 798728 | tf_op jit(solution)/shard_map/ppermute | solution.py:370
  69.9 18.4 %collective-permute-start.13 = (s16[1040,128]{1,0:T(8,128)(2,1)S(1)}, s16[1040,128]{1,0:T(8,128)(2,1)S(1)}, u32[]{:S(2)}, u32[]{:S(2)}) collective-permute-start(s16[1040,128]{1,0:T(8,128)(2,1)S(1)} %get-tuple-element.104), channel_id=1, source_target_pairs={{0,6},{2,0},{4,2},{6,4},{1,7},{3,1},{5,3},{7,5},{8,14},{10,8},{12,... | collective-permute-start | bytes 798728 | tf_op jit(solution)/shard_map/ppermute | solution.py:370
  73.5 13.5 %all-to-all-start.1 = ((s32[32,1,128]{2,1,0:T(1,128)}), s32[32,1,128]{2,1,0:T(1,128)S(1)}, u32[]{:S(2)}, u32[]{:S(2)}) async-start(s32[32,1,128]{2,1,0:T(1,128)} %broadcast_in_dim.14), calls=%async_computation.1 | async-start | bytes 32768 | tf_op jit(solution)/shard_map/all_to_all | solution.py:389

commit v2 on v1

v2 whole, which is shorter than its diff:
```python
import functools

import jax
import jax.numpy as jnp
from jax import lax
from jax.experimental import pallas as pl
from jax.experimental.pallas import tpu as pltpu
from jax.sharding import Mesh
from jax.sharding import PartitionSpec as P


I32 = jnp.int32
F32 = jnp.float32
BF16 = jnp.bfloat16
ROWS = ("r0", "r1")
INNER = ("x", "core")
EVERY = ROWS + INNER
FIRST = ("r0", "x", "core")
SECOND = "r1"
LANES = 128
PACK = 20
STEPS = 256.0
TOP = 32766.0
UNROLL = 4
HEAD = 8


def slot_words(r_ref, c_ref, kinds, keys, count):
    for c in range(count):
        used = jnp.zeros_like(keys)
        fed = jnp.zeros_like(keys)
        for n in range(count):
            used = jnp.where(keys == r_ref[c, n], n + 1, used)
            fed = jnp.where(kinds == c_ref[c, n], n + 1, fed)
        yield c, used, fed


def plan_kernel(wants_ref, win_ref, list_ref, words, table, sem, *, fine, groups, blocks):
    slots = win_ref.shape[1]
    rows = wants_ref.shape[1]
    row = lax.axis_index(ROWS)
    group = lax.axis_index(INNER)
    lane = lax.broadcasted_iota(I32, (slots, LANES), 1)
    half = rows // 2
    for src in range(3):
        first = (row - 1 + src) * (groups * fine) + group * fine
        block = jnp.clip(lax.div(first + LANES, LANES) - 1, 0, blocks - 1)
        keys = block * LANES + lane
        own = (keys >= first) & (keys < first + fine)
        packed = [jnp.zeros((slots, LANES), I32), jnp.zeros((slots, LANES), I32)]
        for c, used, fed in slot_words(wants_ref.at[0], wants_ref.at[1], win_ref[src], keys, rows):
            code = jnp.where(own & (used > 0) & (fed > 0), (fed - 1) * rows + used, 0)
            packed[c // half] = packed[c // half] | (code << (7 * (c % half)))
        words[src, 0, :slots] = packed[0]
        words[src, 1, :slots] = packed[1]
        slot = lax.broadcasted_iota(I32, (slots, LANES), 0)
        marks = jnp.where((packed[0] | packed[1]) != 0, jnp.left_shift(1, slot), 0)
        words[src, 0, slots : slots + 1] = jnp.sum(marks, axis=0, keepdims=True)
    copy = pltpu.make_async_copy(words, table, sem)
    copy.start()
    copy.wait()

    n = jnp.int32(HEAD)
    for src in range(3):
        first = (row - 1 + src) * (groups * fine) + group * fine
        base = lax.rem(first + LANES, LANES)
        began = n

        def fine_row(q, carry, src=src, base=base):
            n, place = carry
            mark = table[src, 0, slots, base + q]

            def found(n, place):
                for t in range(slots):

                    def pairs(n, place, t=t):
                        spot = (q * slots + t) * 64 + place
                        low = table[src, 0, t, base + q]
                        high = table[src, 1, t, base + q]
                        for c in range(rows):
                            code = ((low if c < half else high) >> (7 * (c % half))) & 127
                            list_ref[n] = spot * 512 + c * 64 + jnp.maximum(code - 1, 0)
                            n = n + (code > 0).astype(I32)
                        return n, place + 1

                    n, place = lax.cond((mark & (1 << t)) != 0, pairs, lambda n, place: (n, place), n, place)
                return n, place

            return lax.cond(mark != 0, found, lambda n, place: (n, place), n, place)

        n, _ = lax.fori_loop(0, fine, fine_row, (n, jnp.int32(0)))
        list_ref[src] = n - began


def pack_kernel(
    up_ref, down_ref, counts_ref, win_ref, a_ref, up_out, down_out, told_ref, need, flags, counts, sem, count_sem, copy_sem, *, fine, groups, blocks
):
    slots = win_ref.shape[0]
    rows = up_ref.shape[1]
    pack = up_out.shape[0]
    load = pltpu.make_async_copy(counts_ref, counts, count_sem)
    load.start()
    row = lax.axis_index(ROWS)
    group = lax.axis_index(INNER)
    first = row * (groups * fine) + group * fine
    base = lax.rem(first, LANES)
    lane = lax.broadcasted_iota(I32, (slots, LANES), 1)
    slot = lax.broadcasted_iota(I32, (slots, LANES), 0)
    keys = first - base + lane
    own = (keys >= first) & (keys < first + fine)
    for side, ref in enumerate((up_ref, down_ref)):
        wanted = jnp.zeros((slots, LANES), I32)
        for _, used, fed in slot_words(ref.at[0], ref.at[1], win_ref[...], keys, rows):
            wanted = jnp.where(own & (used > 0) & (fed > 0), jnp.left_shift(1, slot), wanted)
        need[side : side + 1] = jnp.sum(wanted, axis=0, keepdims=True)
    copy = pltpu.make_async_copy(need, flags, sem)
    copy.start()
    copy.wait()
    outs = (up_out, down_out)

    def fine_row(q, places):
        after = []
        for side in range(2):
            mark = flags[side, base + q]
            place = places[side]

            def found(place, side=side, mark=mark):
                for t in range(slots):
                    flag = lax.shift_right_logical(mark, t) & 1

                    @pl.when((flag > 0) & (place < pack))
                    def _(t=t, place=place):
                        pltpu.make_async_copy(a_ref.at[q, t], outs[side].at[place], copy_sem).start()

                    place = place + flag
                return place

            after.append(lax.cond(mark != 0, found, lambda place: place, place))
        return tuple(after)

    up_count, down_count = lax.fori_loop(0, fine, fine_row, (jnp.int32(0), jnp.int32(0)))

    load.wait()
    total = counts[0]
    for c in range(1, rows):
        total = total + counts[c]
    lane = lax.broadcasted_iota(I32, (1, LANES), 1)
    mine = jnp.where((lane == row) & (group == 0), total, 0)
    over = (jnp.maximum(up_count, down_count) > pack).astype(I32)
    words = jnp.where(lane == blocks, over, mine)
    for i in range(told_ref.shape[0]):
        told_ref[i] = words

    @pl.loop(0, jnp.minimum(up_count, pack) + jnp.minimum(down_count, pack))
    def _(i):
        pltpu.make_async_copy(a_ref.at[0, 0], up_out.at[0], copy_sem).wait()


def product_kernel(list_ref, r_ref, own_ref, low_ref, high_ref, keep_ref, send_ref, *, whole):
    pack = low_ref.shape[0]
    cells = keep_ref.shape[0] - 1
    rows = r_ref.shape[0]
    core = lax.axis_index("core")

    @pl.loop(0, cells)
    def _(i):
        keep_ref[i] = jnp.zeros(keep_ref.shape[1:], F32)
        send_ref[i] = jnp.zeros(send_ref.shape[1:], F32)

    begin = jnp.int32(HEAD)
    for src, ref in enumerate((low_ref, own_ref, high_ref)):
        end = begin + list_ref[src]

        @pl.loop(0, lax.div(end - begin + UNROLL - 1, UNROLL))
        def _(i, src=src, ref=ref, begin=begin, end=end):
            for u in range(UNROLL):
                at = begin + i * UNROLL + u
                entry = list_ref[at]
                spot = lax.shift_right_logical(entry, 15) & 63
                place = lax.shift_right_logical(entry, 9) & 63
                row = lax.shift_right_logical(entry, 6) & 7
                slot = lax.shift_right_logical(entry, 3) & 7
                live = at < end
                if src == 1 or whole:
                    place = spot
                else:
                    live = live & (place < pack)
                place = jnp.where(live, place, 0)
                cell = lax.shift_right_logical(slot, 1) * rows + row
                kept = (slot & 1) == core
                part = jnp.dot(r_ref[row, entry & 7], ref[place], preferred_element_type=F32)
                mine = jnp.where(live & kept, cell, cells)
                theirs = jnp.where(live & jnp.logical_not(kept), cell, cells)
                keep_ref[mine] = keep_ref[mine] + part
                send_ref[theirs] = send_ref[theirs] + part

        begin = end


def code_kernel(keep_ref, got_ref, own_out, out):
    rows, size = own_out.shape[:2]
    here = pl.program_id(0) == lax.axis_index("x")

    @pl.when(here)
    def _():
        own_out[...] = keep_ref[...] + got_ref[...]

    @pl.when(jnp.logical_not(here))
    def _():
        levels = []
        for c in range(rows):
            value = keep_ref[c] + got_ref[c]
            top = jnp.max(jnp.abs(value), axis=0, keepdims=True)
            level = jnp.ceil(jnp.log2(jnp.maximum(top, 1e-30)) * STEPS) + 1.0
            code = jnp.round(value * (jnp.exp2(level * (-1.0 / STEPS)) * TOP))
            out[0, pl.ds(c * size, size)] = code.astype(I32).astype(jnp.int16)
            levels.append(level)
        levels = jnp.concatenate(levels + levels, axis=0)
        out[0, pl.ds(rows * size, 2 * rows)] = levels.astype(I32).astype(jnp.int16)


def decode_kernel(own_ref, code_ref, out_ref):
    rows = out_ref.shape[0]
    size = out_ref.shape[2]
    chip = lax.axis_index("x")
    parts = range(code_ref.shape[0])
    scales = [
        jnp.exp2(code_ref[p, pl.ds(rows * size, 2 * rows)].astype(F32) * (1.0 / STEPS)) * (1.0 / TOP) for p in parts
    ]
    for c in range(rows):
        total = own_ref[c]
        for p in parts:
            value = code_ref[p, pl.ds(c * size, size)].astype(F32) * scales[p][c : c + 1]
            total = total + jnp.where(p == chip, 0.0, value)
        out_ref[c, 0] = total.astype(BF16)


def offset_kernel(counts_ref, parts_ref, out_ref, over_ref, *, blocks):
    row = lax.axis_index(ROWS)
    words = parts_ref[...]
    lane = lax.broadcasted_iota(I32, words.shape, 1)
    over_ref[0] = jnp.sum(jnp.where(lane == blocks, words, 0))
    offset = jnp.sum(jnp.where(lane < row, words, 0))
    for c in range(out_ref.shape[0]):
        out_ref[c] = offset
        offset = offset + counts_ref[c]


def smem():
    return pl.BlockSpec(memory_space=pltpu.SMEM)


def vmem():
    return pl.BlockSpec(memory_space=pltpu.VMEM)


def anywhere():
    return pl.BlockSpec(memory_space=pl.ANY)


def shape(dims, dtype):
    return jax.ShapeDtypeStruct(dims, dtype)


def body(r_tiles, r_cols, a_tiles, a_cols, c_cols, c_counts):
    fine, op_slots, size, _ = a_tiles.shape
    rows, r_slots = r_tiles.shape[:2]
    groups = lax.axis_size(INNER)
    chips = lax.axis_size("x")
    row_blocks = lax.axis_size(ROWS)
    row = lax.axis_index(ROWS)
    group = lax.axis_index(INNER)
    blocks = a_cols.shape[0] // LANES
    limit = lambda mb: pltpu.CompilerParams(vmem_limit_bytes=mb * 2**20)

    to_next = [(i, i + 1) for i in range(row_blocks - 1)]
    to_last = [(i + 1, i) for i in range(row_blocks - 1)]

    wants = jnp.stack([r_cols, c_cols])
    below = lax.ppermute(wants, ROWS, to_next)
    above = lax.ppermute(wants, ROWS, to_last)

    by_slot = a_cols.T

    def window(block_row):
        first = block_row * (groups * fine) + group * fine
        block = jnp.clip((first + LANES) // LANES - 1, 0, blocks - 1)
        return lax.dynamic_slice(by_slot, (0, block * LANES), (op_slots, LANES))

    own_window = window(row)
    windows = jnp.stack([window(row - 1), own_window, window(row + 1)])
    firsts = lax.axis_size(FIRST)
    own_tiles = a_tiles.reshape(fine * op_slots, size, size)
    sums = shape((chips * rows + 1, size, size), F32)
    coded_rows = rows * size + 2 * rows

    def plan():
        return pl.pallas_call(
            functools.partial(plan_kernel, fine=fine, groups=groups, blocks=blocks),
            in_specs=[smem(), vmem()],
            out_specs=smem(),
            out_shape=shape((rows * r_slots * op_slots + 64,), I32),
            scratch_shapes=[
                pltpu.VMEM((3, 2, 8, LANES), I32),
                pltpu.SMEM((3, 2, 8, LANES), I32),
                pltpu.SemaphoreType.DMA,
            ],
            compiler_params=limit(4),
            name="plan",
        )(wants, windows)

    def packed():
        return pl.pallas_call(
            functools.partial(pack_kernel, fine=fine, groups=groups, blocks=row_blocks),
            in_specs=[smem(), smem(), anywhere(), vmem(), anywhere()],
            out_specs=[anywhere(), anywhere(), vmem()],
            out_shape=[
                shape((PACK, size, size), BF16),
                shape((PACK, size, size), BF16),
                shape((firsts, 1, LANES), I32),
            ],
            scratch_shapes=[
                pltpu.VMEM((8, LANES), I32),
                pltpu.SMEM((8, LANES), I32),
                pltpu.SMEM((rows,), I32),
                pltpu.SemaphoreType.DMA,
                pltpu.SemaphoreType.DMA,
                pltpu.SemaphoreType.DMA,
            ],
            compiler_params=limit(4),
            name="pack",
        )(above, below, c_counts, own_window, a_tiles)

    def product(low, high, whole):
        return pl.pallas_call(
            functools.partial(product_kernel, whole=whole),
            in_specs=[smem()] + [vmem()] * 4,
            out_specs=[vmem(), vmem()],
            out_shape=[sums, sums],
            compiler_params=limit(20),
            name="all_products" if whole else "products",
        )(pairs, r_tiles, own_tiles, low, high)

    def coded(keep, send):
        got = lax.ppermute(send, "core", [(0, 1), (1, 0)])
        chunk = pl.BlockSpec((rows, size, size), lambda i: (i, 0, 0))
        return pl.pallas_call(
            code_kernel,
            grid=(chips,),
            in_specs=[chunk, chunk],
            out_specs=[
                pl.BlockSpec((rows, size, size), lambda i: (0, 0, 0)),
                pl.BlockSpec((1, coded_rows, size), lambda i: (i, 0, 0)),
            ],
            out_shape=[shape((rows, size, size), F32), shape((chips, coded_rows, size), jnp.int16)],
            compiler_params=limit(20),
            name="code",
        )(keep, got)

    def finish(own, codes):
        return pl.pallas_call(
            decode_kernel,
            in_specs=[vmem(), vmem()],
            out_specs=vmem(),
            out_shape=shape((rows, 1, size, size), BF16),
            compiler_params=limit(16),
            name="decode",
        )(own, codes)

    up, down, words = packed()
    low = lax.ppermute(up, ROWS, to_next)
    high = lax.ppermute(down, ROWS, to_last)
    shared = lax.all_to_all(words, FIRST, 0, 0, tiled=True)
    pairs = plan()
    keep, send = product(low, high, False)
    own, codes = coded(keep, send)
    codes = lax.all_to_all(codes, "x", 0, 0, tiled=True)
    shared = lax.psum(jnp.sum(shared, axis=0), SECOND)
    c_tiles = finish(own, codes)
    row_offsets, over = pl.pallas_call(
        functools.partial(offset_kernel, blocks=row_blocks),
        in_specs=[smem(), vmem()],
        out_specs=[smem(), smem()],
        out_shape=[shape((rows,), I32), shape((1,), I32)],
        compiler_params=limit(4),
        name="offsets",
    )(c_counts, shared)

    def redo(state):
        low = lax.ppermute(own_tiles, ROWS, to_next)
        high = lax.ppermute(own_tiles, ROWS, to_last)
        own, codes = coded(*product(low, high, True))
        return jnp.int32(0), finish(own, lax.all_to_all(codes, "x", 0, 0, tiled=True))

    c_tiles = lax.while_loop(lambda state: state[0] > 0, redo, (over[0], c_tiles))[1]
    return (c_tiles, row_offsets)


def solution(mesh):
    finer = Mesh(mesh.devices.reshape(8, mesh.shape["rows"] // 8, mesh.shape["inner"] // 2, 2), EVERY)
    return jax.shard_map(
        body,
        mesh=finer,
        in_specs=(
            P(ROWS, INNER, None, None),
            P(ROWS, INNER),
            P(EVERY, None, None, None),
            P(),
            P(ROWS, None),
            P(ROWS),
        ),
        out_specs=(P(ROWS, INNER, None, None), P(ROWS)),
        check_vma=False,
    )
```

time: 90.7 us -> 93.9 us (1.035)
  the two profiles are of different devices: /device:TPU:8 before, /device:TPU:1 now
where the time goes in v2:
time: 93.9 us; the launch traced here: 93.3 us
  starting transfers between devices  46.2 us (49%)
  Pallas kernels  17.9 us (19%)
  waiting for transfers between devices  14.1 us (15%)
  blocking collectives  11.3 us (12%)
  local copies, waits for them, and re-layouts  1.47 us (2%)
    all_to_all x1, starting transfers between devices, body(): shared = lax.all_to_all(words, FIRST, 0, 0, tiled=True)  21.4 us
    psum x1, blocking collectives, body(): shared = lax.psum(jnp.sum(shared, axis=0), SECOND)  11.3 us
    ppermute x1, starting transfers between devices, coded(): got = lax.ppermute(send, 'core', [(0, 1), (1, 0)])  9.11 us
    all_to_all x1, waiting for transfers between devices, body(): shared = lax.all_to_all(words, FIRST, 0, 0, tiled=True)  5.5 us
    ppermute x1, starting transfers between devices, body(): below = lax.ppermute(wants, ROWS, to_next)  5.44 us
    ppermute x1, waiting for transfers between devices, body(): high = lax.ppermute(down, ROWS, to_last)  5.06 us
    pallas_call x1, Pallas kernels, plan(): pl.pallas_call(functools.partial(plan_kernel, fine=fine, groups=groups, b...  4.59 us
    ppermute x1, starting transfers between devices, body(): low = lax.ppermute(up, ROWS, to_next)  4.21 us
  transfers between devices with their start and end apart: 7, of which 4 were waited for; matrix products, arithmetic and copies ran while one was open for 1% of the time, Pallas kernels for 10%

profile of v2, /device:TPU:1, one launch (start us, length us, event | category | flops | bytes accessed | tf_op | source)
XLA Modules:
  0.0 93.3 jit_solution(12175321018766277542)
XLA Ops:
  0.6 0.7 pad_add_fusion.1.wants_ref
  1.3 1.3 %collective-permute-start.3 = (s32[2,8,8]{2,1,0:T(8,128)S(1)}, s32[2,8,8]{2,1,0:T(8,128)S(1)}, u32[]{:S(2)}, u32[]{:S(2)}) collective-permute-start(s32[2,8,8]{2,1,0:T(8,128)S(1)} %pad_add_fusion.1.wants_ref), channel_id=1, source_target_pairs={{8,0},{16,8},{24,16},{32,24},{40,32},{48,40},{56,48},{64,56},{72,6... | collective-permute-start | bytes 1544 | tf_op jit(solution)/shard_map/ppermute | solution.py:281
  2.6 5.4 %collective-permute-start.4 = (s32[2,8,8]{2,1,0:T(8,128)S(1)}, s32[2,8,8]{2,1,0:T(8,128)S(1)}, u32[]{:S(2)}, u32[]{:S(2)}) collective-permute-start(s32[2,8,8]{2,1,0:T(8,128)S(1)} %pad_add_fusion.1.wants_ref), channel_id=1, source_target_pairs={{0,8},{8,16},{16,24},{24,32},{32,40},{40,48},{48,56},{56,64},{64,7... | collective-permute-start | bytes 1544 | tf_op jit(solution)/shard_map/ppermute | solution.py:280
  8.1 0.8 dynamic-slice_bitcast_fusion.1
  9.0 0.0 collective-permute-done.3.up_ref
  9.0 0.0 collective-permute-done.4.down_ref
  9.0 0.0 copy-start
  9.0 0.7 copy-done
  9.6 0.0 copy-start.2
  9.6 3.2 %pack.1 = (bf16[20,128,128]{2,1,0:T(8,128)(2,1)S(1)}, bf16[20,128,128]{2,1,0:T(8,128)(2,1)S(1)}, s32[64,1,128]{2,1,0:T(1,128)}) custom-call(s32[2,8,8]{2,1,0:T(8,128)S(1)} %collective-permute-done.3.up_ref, s32[2,8,8]{2,1,0:T(8,128)S(1)} %collective-permute-done.4.down_ref, s32[8]{0:T(128)S(1)} %copy-done, s32[7,128]{1,0:T(8,128)S(1)} %get-tuple-element.62.win_ref, ...), custom_call_target="tpu_custom_call" | custom-call | tf_op jit(solution)/shard_map/pack/pallas_call | solution.py:313
  12.8 4.2 %collective-permute-start.5 = (bf16[20,128,128]{2,1,0:T(8,128)(2,1)S(1)}, bf16[20,128,128]{2,1,0:T(8,128)(2,1)S(1)}, u32[]{:S(2)}, u32[]{:S(2)}) collective-permute-start(bf16[20,128,128]{2,1,0:T(8,128)(2,1)S(1)} %get-tuple-element.42), channel_id=1, source_target_pairs={{0,8},{8,16},{16,24},{24,32},{32,40},{40,48},{48,56},{56,64},{64,7... | collective-permute-start | bytes 1966088 | tf_op jit(solution)/shard_map/ppermute | solution.py:371
  17.1 1.3 %collective-permute-start.6 = (bf16[20,128,128]{2,1,0:T(8,128)(2,1)S(1)}, bf16[20,128,128]{2,1,0:T(8,128)(2,1)S(1)}, u32[]{:S(2)}, u32[]{:S(2)}) collective-permute-start(bf16[20,128,128]{2,1,0:T(8,128)(2,1)S(1)} %get-tuple-element.43), channel_id=1, source_target_pairs={{8,0},{16,8},{24,16},{32,24},{40,32},{48,40},{56,48},{64,56},{72,6... | collective-permute-start | bytes 1966088 | tf_op jit(solution)/shard_map/ppermute | solution.py:372
  18.4 4.6 %plan.1.list_ref = s32[512]{0:T(512)S(1)} custom-call(s32[2,8,8]{2,1,0:T(8,128)S(1)} %pad_add_fusion.1.wants_ref, s32[3,7,128]{2,1,0:T(8,128)S(1)} %pad_add_fusion.win_ref), custom_call_target="tpu_custom_call" | custom-call | tf_op jit(solution)/shard_map/plan/pallas_call | solution.py:298
  23.0 1.6 %collective-permute-done.5.low_ref = bf16[20,128,128]{2,1,0:T(8,128)(2,1)S(1)} collective-permute-done((bf16[20,128,128]{2,1,0:T(8,128)(2,1)S(1)}, bf16[20,128,128]{2,1,0:T(8,128)(2,1)S(1)}, u32[]{:S(2)}, u32[]{:S(2)}) %collective-permute-start.5) | collective-permute-done | bytes 655392 | tf_op jit(solution)/shard_map/ppermute | solution.py:371
  24.5 5.1 %collective-permute-done.6.high_ref = bf16[20,128,128]{2,1,0:T(8,128)(2,1)S(1)} collective-permute-done((bf16[20,128,128]{2,1,0:T(8,128)(2,1)S(1)}, bf16[20,128,128]{2,1,0:T(8,128)(2,1)S(1)}, u32[]{:S(2)}, u32[]{:S(2)}) %collective-permute-start.6) | collective-permute-done | bytes 655392 | tf_op jit(solution)/shard_map/ppermute | solution.py:372
  29.6 0.0 copy-done.2
  29.6 4.1 %products.1 = (f32[33,128,128]{2,1,0:T(8,128)S(1)}, f32[33,128,128]{2,1,0:T(8,128)}) custom-call(s32[512]{0:T(512)S(1)} %plan.1.list_ref, bf16[8,8,128,128]{3,2,1,0:T(8,128)(2,1)} %r_ref.1, bf16[56,128,128]{2,1,0:T(8,128)(2,1)S(1)} %bitcast.18, bf16[20,128,128]{2,1,0:T(8,128)(2,1)S(1)} %collective-permute-done.5.low_ref, ...), custom_call_target="tpu_custom_call" | custom-call | tf_op jit(solution)/shard_map/products/pallas_call | solution.py:335
  33.7 9.1 %collective-permute-start.7 = (f32[33,128,128]{2,1,0:T(8,128)}, f32[33,128,128]{2,1,0:T(8,128)}, u32[]{:S(2)}, u32[]{:S(2)}) collective-permute-start(f32[33,128,128]{2,1,0:T(8,128)} %get-tuple-element.45), channel_id=1, source_target_pairs={{0,1},{1,0},{2,3},{3,2},{4,5},{5,4},{6,7},{7,6},{8,9},{9,8},{10,11... | collective-permute-start | bytes 6488072 | tf_op jit(solution)/shard_map/ppermute | solution.py:345
  42.8 21.4 %all-to-all-start.1 = ((s32[64,1,128]{2,1,0:T(1,128)}), s32[64,1,128]{2,1,0:T(1,128)S(1)}, u32[]{:S(2)}, u32[]{:S(2)}) async-start(s32[64,1,128]{2,1,0:T(1,128)} %get-tuple-element.40), calls=%async_computation.1 | async-start | bytes 65536 | tf_op jit(solution)/shard_map/all_to_all | solution.py:373
  64.2 0.0 collective-permute-done.7.got_ref
  64.2 3.8 %code.3 = (f32[8,128,128]{2,1,0:T(8,128)S(1)}, s16[4,1040,128]{2,1,0:T(8,128)(2,1)}) custom-call(f32[33,128,128]{2,1,0:T(8,128)S(1)} %get-tuple-element.44.keep_ref, f32[33,128,128]{2,1,0:T(8,128)} %collective-permute-done.7.got_ref), custom_call_target="tpu_custom_call" | custom-call | tf_op jit(solution)/shard_map/code/pallas_call | solution.py:347
  68.0 0.0 copy-start.1
  68.0 0.0 copy-start.3
  68.0 5.5 %all-to-all-done.1 = s32[64,1,128]{2,1,0:T(1,128)S(1)} async-done(((s32[64,1,128]{2,1,0:T(1,128)}), s32[64,1,128]{2,1,0:T(1,128)S(1)}, u32[]{:S(2)}, u32[]{:S(2)}) %all-to-all-start.1) | async-done | bytes 32800 | tf_op jit(solution)/shard_map/all_to_all | solution.py:373
  73.5 3.5 %all-to-all-start.2 = ((s16[4,1040,128]{2,1,0:T(8,128)(2,1)}), s16[4,1040,128]{2,1,0:T(8,128)(2,1)S(1)}, u32[]{:S(2)}, u32[]{:S(2)}) async-start(s16[4,1040,128]{2,1,0:T(8,128)(2,1)} %get-tuple-element.47), calls=%async_computation.2 | async-start | bytes 2129920 | tf_op jit(solution)/shard_map/all_to_all | solution.py:377
  77.0 0.1 reduce_sum.11
  77.1 11.3 %psum.7.parts_ref = s32[1,128]{1,0:T(1,128)S(1)} all-reduce(s32[1,128]{1,0:T(1,128)S(1)} %bitcast.22), channel_id=1, replica_groups=mesh['r0'=8,'r1'=8,'x'=4,'core'=2] {'r1'}, use_global_device_ids=true, to_apply=%region_1.2 | all-reduce | flops 128 | bytes 1024 | tf_op jit(solution)/shard_map/psum | solution.py:378
  88.4 0.0 copy-done.1
  88.4 1.2 %offsets.1 = (s32[8]{0:T(128)}, s32[1]{0:T(128)}) custom-call(s32[8]{0:T(128)S(1)} %copy-done.1, s32[1,128]{1,0:T(1,128)S(1)} %psum.7.parts_ref), custom_call_target="tpu_custom_call" | custom-call | tf_op jit(solution)/shard_map/offsets/pallas_call | solution.py:380
  89.6 2.0 %all-to-all-done.2.code_ref = s16[4,1040,128]{2,1,0:T(8,128)(2,1)S(1)} async-done(((s16[4,1040,128]{2,1,0:T(8,128)(2,1)}), s16[4,1040,128]{2,1,0:T(8,128)(2,1)S(1)}, u32[]{:S(2)}, u32[]{:S(2)}) %all-to-all-start.2) | async-done | bytes 1064992 | tf_op jit(solution)/shard_map/all_to_all | solution.py:377
  91.7 1.1 %decode.3 = bf16[8,1,128,128]{3,2,1,0:T(8,128)(2,1)} custom-call(f32[8,128,128]{2,1,0:T(8,128)S(1)} %get-tuple-element.46.own_ref, s16[4,1040,128]{2,1,0:T(8,128)(2,1)S(1)} %all-to-all-done.2.code_ref), custom_call_target="tpu_custom_call" | custom-call | tf_op jit(solution)/shard_map/decode/pallas_call | solution.py:361
  92.7 0.0 copy-done.3
  92.7 0.6 while.9
  (1 shorter events, 0.0 us)
Async XLA Ops:
  1.3 7.6 %collective-permute-start.3 = (s32[2,8,8]{2,1,0:T(8,128)S(1)}, s32[2,8,8]{2,1,0:T(8,128)S(1)}, u32[]{:S(2)}, u32[]{:S(2)}) collective-permute-start(s32[2,8,8]{2,1,0:T(8,128)S(1)} %pad_add_fusion.1.wants_ref), channel_id=1, source_target_pairs={{8,0},{16,8},{24,16},{32,24},{40,32},{48,40},{56,48},{64,56},{72,6... | collective-permute-start | bytes 1544 | tf_op jit(solution)/shard_map/ppermute | solution.py:281
  2.6 6.3 %collective-permute-start.4 = (s32[2,8,8]{2,1,0:T(8,128)S(1)}, s32[2,8,8]{2,1,0:T(8,128)S(1)}, u32[]{:S(2)}, u32[]{:S(2)}) collective-permute-start(s32[2,8,8]{2,1,0:T(8,128)S(1)} %pad_add_fusion.1.wants_ref), channel_id=1, source_target_pairs={{0,8},{8,16},{16,24},{24,32},{32,40},{40,48},{48,56},{56,64},{64,7... | collective-permute-start | bytes 1544 | tf_op jit(solution)/shard_map/ppermute | solution.py:280
  9.0 0.7 copy-start
  9.6 20.0 %copy-start.2 = (bf16[8,7,128,128]{3,2,1,0:T(8,128)(2,1)S(1)}, bf16[8,7,128,128]{3,2,1,0:T(8,128)(2,1)}, u32[]{:S(2)}) copy-start(bf16[8,7,128,128]{3,2,1,0:T(8,128)(2,1)} %a_ref.1) | copy-start | bytes 5505028
  12.8 11.7 %collective-permute-start.5 = (bf16[20,128,128]{2,1,0:T(8,128)(2,1)S(1)}, bf16[20,128,128]{2,1,0:T(8,128)(2,1)S(1)}, u32[]{:S(2)}, u32[]{:S(2)}) collective-permute-start(bf16[20,128,128]{2,1,0:T(8,128)(2,1)S(1)} %get-tuple-element.42), channel_id=1, source_target_pairs={{0,8},{8,16},{16,24},{24,32},{32,40},{40,48},{48,56},{56,64},{64,7... | collective-permute-start | bytes 1966088 | tf_op jit(solution)/shard_map/ppermute | solution.py:371
  17.1 12.5 %collective-permute-start.6 = (bf16[20,128,128]{2,1,0:T(8,128)(2,1)S(1)}, bf16[20,128,128]{2,1,0:T(8,128)(2,1)S(1)}, u32[]{:S(2)}, u32[]{:S(2)}) collective-permute-start(bf16[20,128,128]{2,1,0:T(8,128)(2,1)S(1)} %get-tuple-element.43), channel_id=1, source_target_pairs={{8,0},{16,8},{24,16},{32,24},{40,32},{48,40},{56,48},{64,56},{72,6... | collective-permute-start | bytes 1966088 | tf_op jit(solution)/shard_map/ppermute | solution.py:372
  33.7 30.5 %collective-permute-start.7 = (f32[33,128,128]{2,1,0:T(8,128)}, f32[33,128,128]{2,1,0:T(8,128)}, u32[]{:S(2)}, u32[]{:S(2)}) collective-permute-start(f32[33,128,128]{2,1,0:T(8,128)} %get-tuple-element.45), channel_id=1, source_target_pairs={{0,1},{1,0},{2,3},{3,2},{4,5},{5,4},{6,7},{7,6},{8,9},{9,8},{10,11... | collective-permute-start | bytes 6488072 | tf_op jit(solution)/shard_map/ppermute | solution.py:345
  42.8 30.7 %all-to-all-start.1 = ((s32[64,1,128]{2,1,0:T(1,128)}), s32[64,1,128]{2,1,0:T(1,128)S(1)}, u32[]{:S(2)}, u32[]{:S(2)}) async-start(s32[64,1,128]{2,1,0:T(1,128)} %get-tuple-element.40), calls=%async_computation.1 | async-start | bytes 65536 | tf_op jit(solution)/shard_map/all_to_all | solution.py:373
  68.0 20.5 %copy-start.1 = (s32[8]{0:T(128)S(1)}, s32[8]{0:T(128)}, u32[]{:S(2)}) copy-start(s32[8]{0:T(128)} %counts_ref.3) | copy-start | bytes 100
  68.0 24.7 %copy-start.3 = (bf16[8,7,128,128]{3,2,1,0:T(8,128)(2,1)S(1)}, bf16[8,7,128,128]{3,2,1,0:T(8,128)(2,1)}, u32[]{:S(2)}) copy-start(bf16[8,7,128,128]{3,2,1,0:T(8,128)(2,1)} %a_ref.1) | copy-start | bytes 5505028
  73.5 18.2 %all-to-all-start.2 = ((s16[4,1040,128]{2,1,0:T(8,128)(2,1)}), s16[4,1040,128]{2,1,0:T(8,128)(2,1)S(1)}, u32[]{:S(2)}, u32[]{:S(2)}) async-start(s16[4,1040,128]{2,1,0:T(8,128)(2,1)} %get-tuple-element.47), calls=%async_computation.2 | async-start | bytes 2129920 | tf_op jit(solution)/shard_map/all_to_all | solution.py:377

commit v3 on v2

--- a/solution.py
+++ b/solution.py
@@ -23,21 +23,31 @@
 TOP = 32766.0
 UNROLL = 4
 HEAD = 8
-
-
-def slot_words(r_ref, c_ref, kinds, keys, count):
+HALF = 512
+
+
+def slot_words(wants_ref, kinds, keys, count):
     for c in range(count):
         used = jnp.zeros_like(keys)
         fed = jnp.zeros_like(keys)
         for n in range(count):
-            used = jnp.where(keys == r_ref[c, n], n + 1, used)
-            fed = jnp.where(kinds == c_ref[c, n], n + 1, fed)
+            used = jnp.where(keys == wants_ref[c, n], n + 1, used)
+            fed = jnp.where(kinds == wants_ref[count + c, n], n + 1, fed)
         yield c, used, fed
 
 
-def plan_kernel(wants_ref, win_ref, list_ref, words, table, sem, *, fine, groups, blocks):
+def plan_kernel(
+    wants_ref, win_ref, r_ref, a_ref, list_ref, r_out, a_out, words, table, sem, load_sems, *, fine, groups, blocks
+):
+    loads = [
+        pltpu.make_async_copy(r_ref, r_out, load_sems.at[0]),
+        pltpu.make_async_copy(a_ref, a_out, load_sems.at[1]),
+    ]
+    for load in loads:
+        load.start()
     slots = win_ref.shape[1]
     rows = wants_ref.shape[1]
+    core = lax.axis_index("core")
     row = lax.axis_index(ROWS)
     group = lax.axis_index(INNER)
     lane = lax.broadcasted_iota(I32, (slots, LANES), 1)
@@ -48,7 +58,7 @@
         keys = block * LANES + lane
         own = (keys >= first) & (keys < first + fine)
         packed = [jnp.zeros((slots, LANES), I32), jnp.zeros((slots, LANES), I32)]
-        for c, used, fed in slot_words(wants_ref.at[0], wants_ref.at[1], win_ref[src], keys, rows):
+        for c, used, fed in slot_words(wants_ref, win_ref[src], keys, rows):
             code = jnp.where(own & (used > 0) & (fed > 0), (fed - 1) * rows + used, 0)
             packed[c // half] = packed[c // half] | (code << (7 * (c % half)))
         words[src, 0, :slots] = packed[0]
@@ -60,46 +70,50 @@
     copy.start()
     copy.wait()
 
-    n = jnp.int32(HEAD)
+    n = (jnp.int32(HEAD), jnp.int32(HALF))
     for src in range(3):
         first = (row - 1 + src) * (groups * fine) + group * fine
         base = lax.rem(first + LANES, LANES)
         began = n
 
         def fine_row(q, carry, src=src, base=base):
-            n, place = carry
             mark = table[src, 0, slots, base + q]
 
-            def found(n, place):
+            def found(carry):
                 for t in range(slots):
 
-                    def pairs(n, place, t=t):
+                    def pairs(carry, t=t):
+                        sent, kept, place = carry
                         spot = (q * slots + t) * 64 + place
                         low = table[src, 0, t, base + q]
                         high = table[src, 1, t, base + q]
                         for c in range(rows):
-                            code = ((low if c < half else high) >> (7 * (c % half))) & 127
-                            list_ref[n] = spot * 512 + c * 64 + jnp.maximum(code - 1, 0)
-                            n = n + (code > 0).astype(I32)
-                        return n, place + 1
-
-                    n, place = lax.cond((mark & (1 << t)) != 0, pairs, lambda n, place: (n, place), n, place)
-                return n, place
-
-            return lax.cond(mark != 0, found, lambda n, place: (n, place), n, place)
-
-        n, _ = lax.fori_loop(0, fine, fine_row, (n, jnp.int32(0)))
-        list_ref[src] = n - began
+                            code = (((low if c < half else high) >> (7 * (c % half))) & 127) - 1
+                            mine = ((code >> 3) & 1) == core
+                            list_ref[jnp.where(mine, kept, sent)] = spot * 512 + c * 64 + jnp.maximum(code, 0)
+                            live = code >= 0
+                            kept = kept + (live & mine).astype(I32)
+                            sent = sent + (live & jnp.logical_not(mine)).astype(I32)
+                        return sent, kept, place + 1
+
+                    carry = lax.cond((mark & (1 << t)) != 0, pairs, lambda carry: carry, carry)
+                return carry
+
+            return lax.cond(mark != 0, found, lambda carry: carry, carry)
+
+        n = lax.fori_loop(0, fine, fine_row, (*n, jnp.int32(0)))[:2]
+        list_ref[src] = n[0] - began[0]
+        list_ref[3 + src] = n[1] - began[1]
+    for load in loads:
+        load.wait()
 
 
 def pack_kernel(
-    up_ref, down_ref, counts_ref, win_ref, a_ref, up_out, down_out, told_ref, need, flags, counts, sem, count_sem, copy_sem, *, fine, groups, blocks
+    up_ref, down_ref, wants_ref, win_ref, a_ref, up_out, down_out, told_ref, need, flags, sem, copy_sem, *, fine, groups, blocks
 ):
     slots = win_ref.shape[0]
     rows = up_ref.shape[1]
     pack = up_out.shape[0]
-    load = pltpu.make_async_copy(counts_ref, counts, count_sem)
-    load.start()
     row = lax.axis_index(ROWS)
     group = lax.axis_index(INNER)
     first = row * (groups * fine) + group * fine
@@ -110,7 +124,7 @@
     own = (keys >= first) & (keys < first + fine)
     for side, ref in enumerate((up_ref, down_ref)):
         wanted = jnp.zeros((slots, LANES), I32)
-        for _, used, fed in slot_words(ref.at[0], ref.at[1], win_ref[...], keys, rows):
+        for _, used, fed in slot_words(ref, win_ref[...], keys, rows):
             wanted = jnp.where(own & (used > 0) & (fed > 0), jnp.left_shift(1, slot), wanted)
         need[side : side + 1] = jnp.sum(wanted, axis=0, keepdims=True)
     copy = pltpu.make_async_copy(need, flags, sem)
@@ -140,36 +154,32 @@
 
     up_count, down_count = lax.fori_loop(0, fine, fine_row, (jnp.int32(0), jnp.int32(0)))
 
-    load.wait()
-    total = counts[0]
+    total = wants_ref[2 * rows, 0]
     for c in range(1, rows):
-        total = total + counts[c]
+        total = total + wants_ref[2 * rows, c]
     lane = lax.broadcasted_iota(I32, (1, LANES), 1)
     mine = jnp.where((lane == row) & (group == 0), total, 0)
     over = (jnp.maximum(up_count, down_count) > pack).astype(I32)
     words = jnp.where(lane == blocks, over, mine)
-    for i in range(told_ref.shape[0]):
-        told_ref[i] = words
+    told_ref[...] = words
 
     @pl.loop(0, jnp.minimum(up_count, pack) + jnp.minimum(down_count, pack))
     def _(i):
         pltpu.make_async_copy(a_ref.at[0, 0], up_out.at[0], copy_sem).wait()
 
 
-def product_kernel(list_ref, r_ref, own_ref, low_ref, high_ref, keep_ref, send_ref, *, whole):
+def product_kernel(list_ref, r_ref, own_ref, low_ref, high_ref, out_ref, *, side, whole):
     pack = low_ref.shape[0]
-    cells = keep_ref.shape[0] - 1
+    cells = out_ref.shape[0] - 1
     rows = r_ref.shape[0]
-    core = lax.axis_index("core")
 
     @pl.loop(0, cells)
     def _(i):
-        keep_ref[i] = jnp.zeros(keep_ref.shape[1:], F32)
-        send_ref[i] = jnp.zeros(send_ref.shape[1:], F32)
-
-    begin = jnp.int32(HEAD)
+        out_ref[i] = jnp.zeros(out_ref.shape[1:], F32)
+
+    begin = jnp.int32(HALF if side else HEAD)
     for src, ref in enumerate((low_ref, own_ref, high_ref)):
-        end = begin + list_ref[src]
+        end = begin + list_ref[3 * side + src]
 
         @pl.loop(0, lax.div(end - begin + UNROLL - 1, UNROLL))
         def _(i, src=src, ref=ref, begin=begin, end=end):
@@ -186,13 +196,9 @@
                 else:
                     live = live & (place < pack)
                 place = jnp.where(live, place, 0)
-                cell = lax.shift_right_logical(slot, 1) * rows + row
-                kept = (slot & 1) == core
+                cell = jnp.where(live, lax.shift_right_logical(slot, 1) * rows + row, cells)
                 part = jnp.dot(r_ref[row, entry & 7], ref[place], preferred_element_type=F32)
-                mine = jnp.where(live & kept, cell, cells)
-                theirs = jnp.where(live & jnp.logical_not(kept), cell, cells)
-                keep_ref[mine] = keep_ref[mine] + part
-                send_ref[theirs] = send_ref[theirs] + part
+                out_ref[cell] = out_ref[cell] + part
 
         begin = end
 
@@ -264,7 +270,7 @@
 
 def body(r_tiles, r_cols, a_tiles, a_cols, c_cols, c_counts):
     fine, op_slots, size, _ = a_tiles.shape
-    rows, r_slots = r_tiles.shape[:2]
+    rows, _ = r_tiles.shape[:2]
     groups = lax.axis_size(INNER)
     chips = lax.axis_size("x")
     row_blocks = lax.axis_size(ROWS)
@@ -276,7 +282,7 @@
     to_next = [(i, i + 1) for i in range(row_blocks - 1)]
     to_last = [(i + 1, i) for i in range(row_blocks - 1)]
 
-    wants = jnp.stack([r_cols, c_cols])
+    wants = jnp.concatenate([r_cols, c_cols, c_counts[None]])
     below = lax.ppermute(wants, ROWS, to_next)
     above = lax.ppermute(wants, ROWS, to_last)
 
@@ -297,52 +303,60 @@
     def plan():
         return pl.pallas_call(
             functools.partial(plan_kernel, fine=fine, groups=groups, blocks=blocks),
-            in_specs=[smem(), vmem()],
-            out_specs=smem(),
-            out_shape=shape((rows * r_slots * op_slots + 64,), I32),
+            in_specs=[smem(), vmem(), anywhere(), anywhere()],
+            out_specs=[smem(), vmem(), vmem()],
+            out_shape=[
+                shape((2 * HALF,), I32),
+                pltpu.VMEM(r_tiles.shape, BF16),
+                pltpu.VMEM(own_tiles.shape, BF16),
+            ],
             scratch_shapes=[
                 pltpu.VMEM((3, 2, 8, LANES), I32),
                 pltpu.SMEM((3, 2, 8, LANES), I32),
                 pltpu.SemaphoreType.DMA,
+                pltpu.SemaphoreType.DMA((2,)),
             ],
-            compiler_params=limit(4),
+            compiler_params=limit(8),
             name="plan",
-        )(wants, windows)
+        )(wants, windows, r_tiles, own_tiles)
 
     def packed():
         return pl.pallas_call(
             functools.partial(pack_kernel, fine=fine, groups=groups, blocks=row_blocks),
-            in_specs=[smem(), smem(), anywhere(), vmem(), anywhere()],
+            in_specs=[smem(), smem(), smem(), vmem(), anywhere()],
             out_specs=[anywhere(), anywhere(), vmem()],
             out_shape=[
                 shape((PACK, size, size), BF16),
                 shape((PACK, size, size), BF16),
-                shape((firsts, 1, LANES), I32),
+                shape((1, LANES), I32),
             ],
             scratch_shapes=[
                 pltpu.VMEM((8, LANES), I32),
                 pltpu.SMEM((8, LANES), I32),
-                pltpu.SMEM((rows,), I32),
-                pltpu.SemaphoreType.DMA,
                 pltpu.SemaphoreType.DMA,
                 pltpu.SemaphoreType.DMA,
             ],
             compiler_params=limit(4),
             name="pack",
-        )(above, below, c_counts, own_window, a_tiles)
-
-    def product(low, high, whole):
+        )(above, below, wants, own_window, a_tiles)
+
+    def product(low, high, side, whole, near):
         return pl.pallas_call(
-            functools.partial(product_kernel, whole=whole),
+            functools.partial(product_kernel, side=side, whole=whole),
             in_specs=[smem()] + [vmem()] * 4,
-            out_specs=[vmem(), vmem()],
-            out_shape=[sums, sums],
-            compiler_params=limit(20),
-            name="all_products" if whole else "products",
-        )(pairs, r_tiles, own_tiles, low, high)
-
-    def coded(keep, send):
+            out_specs=vmem(),
+            out_shape=sums,
+            compiler_params=limit(16),
+            name="products",
+        )(pairs, *near, low, high)
+
+    def multiplied(low, high, whole, near):
+        send = product(low, high, 0, whole, near)
         got = lax.ppermute(send, "core", [(0, 1), (1, 0)])
+        keep = product(low, high, 1, whole, near)
+        return keep, got
+
+    def coded(keep, got):
         chunk = pl.BlockSpec((rows, size, size), lambda i: (i, 0, 0))
         return pl.pallas_call(
             code_kernel,
@@ -370,10 +384,9 @@
     up, down, words = packed()
     low = lax.ppermute(up, ROWS, to_next)
     high = lax.ppermute(down, ROWS, to_last)
-    shared = lax.all_to_all(words, FIRST, 0, 0, tiled=True)
-    pairs = plan()
-    keep, send = product(low, high, False)
-    own, codes = coded(keep, send)
+    shared = lax.all_to_all(jnp.broadcast_to(words[None], (firsts, 1, LANES)), FIRST, 0, 0, tiled=True)
+    pairs, r_near, own_near = plan()
+    own, codes = coded(*multiplied(low, high, False, (r_near, own_near)))
     codes = lax.all_to_all(codes, "x", 0, 0, tiled=True)
     shared = lax.psum(jnp.sum(shared, axis=0), SECOND)
     c_tiles = finish(own, codes)
@@ -389,7 +402,7 @@
     def redo(state):
         low = lax.ppermute(own_tiles, ROWS, to_next)
         high = lax.ppermute(own_tiles, ROWS, to_last)
-        own, codes = coded(*product(low, high, True))
+        own, codes = coded(*multiplied(low, high, True, (r_tiles, own_tiles)))
         return jnp.int32(0), finish(own, lax.all_to_all(codes, "x", 0, 0, tiled=True))
 
     c_tiles = lax.while_loop(lambda state: state[0] > 0, redo, (over[0], c_tiles))[1]

time: 93.9 us -> 87.6 us (0.933)
  starting transfers between devices: 46.2 us -> 33.4 us
  waiting for transfers between devices: 14.1 us -> 20.3 us
  local copies, waits for them, and re-layouts: 1.47 us -> 3 us
  Pallas kernels: 17.9 us -> 16.9 us
    all_to_all x1, starting transfers between devices: 21.4 us -> 13.3 us  [body(): lax.all_to_all(jnp.broadcast_to(words[None], (firsts, 1, LANES)), FIRST,...]
    ppermute x1, waiting for transfers between devices: 1.56 us -> 6.78 us  [body(): low = lax.ppermute(up, ROWS, to_next)]
    ppermute x1, starting transfers between devices: 9.11 us -> 4.93 us  [multiplied(): got = lax.ppermute(send, 'core', [(0, 1), (1, 0)])]
    all_to_all x1, waiting for transfers between devices: 5.5 us -> 2.66 us  [body(): lax.all_to_all(jnp.broadcast_to(words[None], (firsts, 1, LANES)), FIRST,...]
    ppermute x1, waiting for transfers between devices: 0.01 us -> 2.84 us  [body(): above = lax.ppermute(wants, ROWS, to_last)]
    pallas_call x1 -> x2, Pallas kernels: 4.07 us -> 3.88 us  [product(): pl.pallas_call(functools.partial(product_kernel, side=side, whole=whole),...]
  transfers between devices with their start and end apart: 7 -> 7, of which waited for: 4 -> 5; matrix products, arithmetic and copies ran while one was open for 1% -> 2% of each run, Pallas kernels for 10% -> 12%
where the time goes in v3:
time: 87.6 us; the launch traced here: 87 us
  starting transfers between devices  33.4 us (38%)
  waiting for transfers between devices  20.3 us (23%)
  Pallas kernels  16.9 us (19%)
  blocking collectives  11.1 us (13%)
  local copies, waits for them, and re-layouts  3 us (3%)
    all_to_all x1, starting transfers between devices, body(): lax.all_to_all(jnp.broadcast_to(words[None], (firsts, 1, LANES)), FIRST,...  13.3 us
    psum x1, blocking collectives, body(): shared = lax.psum(jnp.sum(shared, axis=0), SECOND)  11.1 us
    ppermute x1, waiting for transfers between devices, body(): low = lax.ppermute(up, ROWS, to_next)  6.78 us
    ppermute x1, waiting for transfers between devices, body(): high = lax.ppermute(down, ROWS, to_last)  5.73 us
    ppermute x1, starting transfers between devices, multiplied(): got = lax.ppermute(send, 'core', [(0, 1), (1, 0)])  4.93 us
    ppermute x1, starting transfers between devices, body(): below = lax.ppermute(wants, ROWS, to_next)  4.8 us
    ppermute x1, starting transfers between devices, body(): low = lax.ppermute(up, ROWS, to_next)  4.23 us
    pallas_call x1, Pallas kernels, plan(): pl.pallas_call(functools.partial(plan_kernel, fine=fine, groups=groups, b...  4.07 us
  transfers between devices with their start and end apart: 7, of which 5 were waited for; matrix products, arithmetic and copies ran while one was open for 2% of the time, Pallas kernels for 12%

profile of v3, /device:TPU:1, one launch (start us, length us, event | category | flops | bytes accessed | tf_op | source)
XLA Modules:
  0.0 87.0 jit_solution(17280177827902504372)
XLA Ops:
  0.6 0.7 pad_add_fusion.wants_ref
  1.4 4.8 %collective-permute-start.4 = (s32[17,8]{1,0:T(8,128)S(1)}, s32[17,8]{1,0:T(8,128)S(1)}, u32[]{:S(2)}, u32[]{:S(2)}) collective-permute-start(s32[17,8]{1,0:T(8,128)S(1)} %pad_add_fusion.wants_ref), channel_id=1, source_target_pairs={{0,8},{8,16},{16,24},{24,32},{32,40},{40,48},{48,56},{56,64},{64,7... | collective-permute-start | bytes 1640 | tf_op jit(solution)/shard_map/ppermute | solution.py:286
  6.2 1.3 %collective-permute-start.3 = (s32[17,8]{1,0:T(8,128)S(1)}, s32[17,8]{1,0:T(8,128)S(1)}, u32[]{:S(2)}, u32[]{:S(2)}) collective-permute-start(s32[17,8]{1,0:T(8,128)S(1)} %pad_add_fusion.wants_ref), channel_id=1, source_target_pairs={{8,0},{16,8},{24,16},{32,24},{40,32},{48,40},{56,48},{64,56},{72,6... | collective-permute-start | bytes 1640 | tf_op jit(solution)/shard_map/ppermute | solution.py:287
  7.5 0.0 copy-start.3
  7.5 0.9 dynamic-slice_bitcast_fusion.1
  8.4 0.0 collective-permute-done.4.down_ref
  8.4 2.8 %collective-permute-done.3.up_ref = s32[17,8]{1,0:T(8,128)S(1)} collective-permute-done((s32[17,8]{1,0:T(8,128)S(1)}, s32[17,8]{1,0:T(8,128)S(1)}, u32[]{:S(2)}, u32[]{:S(2)}) %collective-permute-start.3) | collective-permute-done | bytes 576 | tf_op jit(solution)/shard_map/ppermute | solution.py:287
  11.2 2.9 %pack.1 = (bf16[20,128,128]{2,1,0:T(8,128)(2,1)S(1)}, bf16[20,128,128]{2,1,0:T(8,128)(2,1)S(1)}, s32[1,128]{1,0:T(1,128)S(1)}) custom-call(s32[17,8]{1,0:T(8,128)S(1)} %collective-permute-done.3.up_ref, s32[17,8]{1,0:T(8,128)S(1)} %collective-permute-done.4.down_ref, s32[17,8]{1,0:T(8,128)S(1)} %pad_add_fusion.wants_ref, ...), custom_call_target="tpu_custom_call" | custom-call | tf_op jit(solution)/shard_map/pack/pallas_call | solution.py:324
  14.2 4.2 %collective-permute-start.5 = (bf16[20,128,128]{2,1,0:T(8,128)(2,1)S(1)}, bf16[20,128,128]{2,1,0:T(8,128)(2,1)S(1)}, u32[]{:S(2)}, u32[]{:S(2)}) collective-permute-start(bf16[20,128,128]{2,1,0:T(8,128)(2,1)S(1)} %get-tuple-element.44), channel_id=1, source_target_pairs={{0,8},{8,16},{16,24},{24,32},{32,40},{40,48},{48,56},{56,64},{64,7... | collective-permute-start | bytes 1966088 | tf_op jit(solution)/shard_map/ppermute | solution.py:385
  18.4 1.3 %collective-permute-start.6 = (bf16[20,128,128]{2,1,0:T(8,128)(2,1)S(1)}, bf16[20,128,128]{2,1,0:T(8,128)(2,1)S(1)}, u32[]{:S(2)}, u32[]{:S(2)}) collective-permute-start(bf16[20,128,128]{2,1,0:T(8,128)(2,1)S(1)} %get-tuple-element.45), channel_id=1, source_target_pairs={{8,0},{16,8},{24,16},{32,24},{40,32},{48,40},{56,48},{64,56},{72,6... | collective-permute-start | bytes 1966088 | tf_op jit(solution)/shard_map/ppermute | solution.py:386
  19.7 0.0 copy-done.3
  19.7 4.1 %plan.1 = (s32[1024]{0:T(1024)S(1)}, bf16[8,8,128,128]{3,2,1,0:T(8,128)(2,1)S(1)}, bf16[56,128,128]{2,1,0:T(8,128)(2,1)S(1)}) custom-call(s32[17,8]{1,0:T(8,128)S(1)} %pad_add_fusion.wants_ref, s32[3,7,128]{2,1,0:T(8,128)S(1)} %pad_add_fusion.1.win_ref, bf16[8,8,128,128]{3,2,1,0:T(8,128)(2,1)} %r_ref.1, bf16[56,128,128]{2,1,0:T(8,128)(2,1)S(1)} %bitcast.21), custom_call_target="tpu_custom_call" | custom-call | tf_op jit(solution)/shard_map/plan/pallas_call | solution.py:304
  23.8 0.0 copy-start
  23.8 6.8 %collective-permute-done.5.low_ref = bf16[20,128,128]{2,1,0:T(8,128)(2,1)S(1)} collective-permute-done((bf16[20,128,128]{2,1,0:T(8,128)(2,1)S(1)}, bf16[20,128,128]{2,1,0:T(8,128)(2,1)S(1)}, u32[]{:S(2)}, u32[]{:S(2)}) %collective-permute-start.5) | collective-permute-done | bytes 655392 | tf_op jit(solution)/shard_map/ppermute | solution.py:385
  30.6 5.7 %collective-permute-done.6.high_ref = bf16[20,128,128]{2,1,0:T(8,128)(2,1)S(1)} collective-permute-done((bf16[20,128,128]{2,1,0:T(8,128)(2,1)S(1)}, bf16[20,128,128]{2,1,0:T(8,128)(2,1)S(1)}, u32[]{:S(2)}, u32[]{:S(2)}) %collective-permute-start.6) | collective-permute-done | bytes 655392 | tf_op jit(solution)/shard_map/ppermute | solution.py:386
  36.3 2.5 %products.7 = f32[33,128,128]{2,1,0:T(8,128)} custom-call(s32[1024]{0:T(1024)S(1)} %get-tuple-element.72.list_ref, bf16[8,8,128,128]{3,2,1,0:T(8,128)(2,1)S(1)} %get-tuple-element.42.r_ref, bf16[56,128,128]{2,1,0:T(8,128)(2,1)S(1)} %get-tuple-element.43.own_ref, bf16[20,128,128]{2,1,0:T(8,128)(2,1)S(1)} %collective-permute-done.5.low_ref, ...), custom_call_target="tpu_custom_call" | custom-call | tf_op jit(solution)/shard_map/products/pallas_call | solution.py:344
  38.8 0.0 copy-done
  38.8 4.9 %collective-permute-start.7 = (f32[33,128,128]{2,1,0:T(8,128)}, f32[33,128,128]{2,1,0:T(8,128)}, u32[]{:S(2)}, u32[]{:S(2)}) collective-permute-start(f32[33,128,128]{2,1,0:T(8,128)} %products.7), channel_id=1, source_target_pairs={{0,1},{1,0},{2,3},{3,2},{4,5},{5,4},{6,7},{7,6},{8,9},{9,8},{10,11... | collective-permute-start | bytes 6488072 | tf_op jit(solution)/shard_map/ppermute | solution.py:355
  43.8 0.6 broadcast_in_dim.13
  44.4 13.3 %all-to-all-start.1 = ((s32[64,1,128]{2,1,0:T(1,128)}), s32[64,1,128]{2,1,0:T(1,128)S(1)}, u32[]{:S(2)}, u32[]{:S(2)}) async-start(s32[64,1,128]{2,1,0:T(1,128)} %broadcast_in_dim.13), calls=%async_computation.1 | async-start | bytes 65536 | tf_op jit(solution)/shard_map/all_to_all | solution.py:387
  57.7 0.0 copy-start.1
  57.7 1.5 %copy-done.1 = bf16[56,128,128]{2,1,0:T(8,128)(2,1)S(1)} copy-done((bf16[56,128,128]{2,1,0:T(8,128)(2,1)S(1)}, bf16[56,128,128]{2,1,0:T(8,128)(2,1)}, u32[]{:S(2)}) %copy-start.1) | copy-done | bytes 1835032
  59.2 1.4 %products.6.keep_ref = f32[33,128,128]{2,1,0:T(8,128)S(1)} custom-call(s32[1024]{0:T(1024)S(1)} %get-tuple-element.72.list_ref, bf16[8,8,128,128]{3,2,1,0:T(8,128)(2,1)S(1)} %get-tuple-element.42.r_ref, bf16[56,128,128]{2,1,0:T(8,128)(2,1)S(1)} %copy-done.1, bf16[20,128,128]{2,1,0:T(8,128)(2,1)S(1)} %collective-permute-done.5.low_ref, ...), custom_call_target="tpu_custom_call" | custom-call | tf_op jit(solution)/shard_map/products/pallas_call | solution.py:344
  60.6 0.0 collective-permute-done.7.got_ref
  60.6 3.8 %code.3 = (f32[8,128,128]{2,1,0:T(8,128)S(1)}, s16[4,1040,128]{2,1,0:T(8,128)(2,1)}) custom-call(f32[33,128,128]{2,1,0:T(8,128)S(1)} %products.6.keep_ref, f32[33,128,128]{2,1,0:T(8,128)} %collective-permute-done.7.got_ref), custom_call_target="tpu_custom_call" | custom-call | tf_op jit(solution)/shard_map/code/pallas_call | solution.py:361
  64.4 0.0 copy-start.2
  64.4 0.0 copy-start.4
  64.4 2.7 %all-to-all-done.1 = s32[64,1,128]{2,1,0:T(1,128)S(1)} async-done(((s32[64,1,128]{2,1,0:T(1,128)}), s32[64,1,128]{2,1,0:T(1,128)S(1)}, u32[]{:S(2)}, u32[]{:S(2)}) %all-to-all-start.1) | async-done | bytes 32800 | tf_op jit(solution)/shard_map/all_to_all | solution.py:387
  67.0 3.5 %all-to-all-start.2 = ((s16[4,1040,128]{2,1,0:T(8,128)(2,1)}), s16[4,1040,128]{2,1,0:T(8,128)(2,1)S(1)}, u32[]{:S(2)}, u32[]{:S(2)}) async-start(s16[4,1040,128]{2,1,0:T(8,128)(2,1)} %get-tuple-element.47), calls=%async_computation.2 | async-start | bytes 2129920 | tf_op jit(solution)/shard_map/all_to_all | solution.py:390
  70.6 11.1 %psum.7.parts_ref = s32[1,128]{1,0:T(1,128)S(1)} all-reduce(s32[1,128]{1,0:T(1,128)S(1)} %bitcast.24), channel_id=1, replica_groups=mesh['r0'=8,'r1'=8,'x'=4,'core'=2] {'r1'}, use_global_device_ids=true, to_apply=%region_1.2 | all-reduce | flops 128 | bytes 1024 | tf_op jit(solution)/shard_map/psum | solution.py:391
  81.7 0.0 copy-done.2
  81.7 1.2 %offsets.1 = (s32[8]{0:T(128)}, s32[1]{0:T(128)}) custom-call(s32[8]{0:T(128)S(1)} %copy-done.2, s32[1,128]{1,0:T(1,128)S(1)} %psum.7.parts_ref), custom_call_target="tpu_custom_call" | custom-call | tf_op jit(solution)/shard_map/offsets/pallas_call | solution.py:393
  82.9 2.3 %all-to-all-done.2.code_ref = s16[4,1040,128]{2,1,0:T(8,128)(2,1)S(1)} async-done(((s16[4,1040,128]{2,1,0:T(8,128)(2,1)}), s16[4,1040,128]{2,1,0:T(8,128)(2,1)S(1)}, u32[]{:S(2)}, u32[]{:S(2)}) %all-to-all-start.2) | async-done | bytes 1064992 | tf_op jit(solution)/shard_map/all_to_all | solution.py:390
  85.2 1.1 %decode.3 = bf16[8,1,128,128]{3,2,1,0:T(8,128)(2,1)} custom-call(f32[8,128,128]{2,1,0:T(8,128)S(1)} %get-tuple-element.46.own_ref, s16[4,1040,128]{2,1,0:T(8,128)(2,1)S(1)} %all-to-all-done.2.code_ref), custom_call_target="tpu_custom_call" | custom-call | tf_op jit(solution)/shard_map/decode/pallas_call | solution.py:375
  86.3 0.0 copy-done.4
  86.3 0.7 while.9
  (2 shorter events, 0.0 us)
Async XLA Ops:
  1.4 7.0 %collective-permute-start.4 = (s32[17,8]{1,0:T(8,128)S(1)}, s32[17,8]{1,0:T(8,128)S(1)}, u32[]{:S(2)}, u32[]{:S(2)}) collective-permute-start(s32[17,8]{1,0:T(8,128)S(1)} %pad_add_fusion.wants_ref), channel_id=1, source_target_pairs={{0,8},{8,16},{16,24},{24,32},{32,40},{40,48},{48,56},{56,64},{64,7... | collective-permute-start | bytes 1640 | tf_op jit(solution)/shard_map/ppermute | solution.py:286
  6.2 5.1 %collective-permute-start.3 = (s32[17,8]{1,0:T(8,128)S(1)}, s32[17,8]{1,0:T(8,128)S(1)}, u32[]{:S(2)}, u32[]{:S(2)}) collective-permute-start(s32[17,8]{1,0:T(8,128)S(1)} %pad_add_fusion.wants_ref), channel_id=1, source_target_pairs={{8,0},{16,8},{24,16},{32,24},{40,32},{48,40},{56,48},{64,56},{72,6... | collective-permute-start | bytes 1640 | tf_op jit(solution)/shard_map/ppermute | solution.py:287
  7.5 12.2 %copy-start.3 = (bf16[8,7,128,128]{3,2,1,0:T(8,128)(2,1)S(1)}, bf16[8,7,128,128]{3,2,1,0:T(8,128)(2,1)}, u32[]{:S(2)}) copy-start(bf16[8,7,128,128]{3,2,1,0:T(8,128)(2,1)} %a_ref.1) | copy-start | bytes 5505028
  14.2 16.4 %collective-permute-start.5 = (bf16[20,128,128]{2,1,0:T(8,128)(2,1)S(1)}, bf16[20,128,128]{2,1,0:T(8,128)(2,1)S(1)}, u32[]{:S(2)}, u32[]{:S(2)}) collective-permute-start(bf16[20,128,128]{2,1,0:T(8,128)(2,1)S(1)} %get-tuple-element.44), channel_id=1, source_target_pairs={{0,8},{8,16},{16,24},{24,32},{32,40},{40,48},{48,56},{56,64},{64,7... | collective-permute-start | bytes 1966088 | tf_op jit(solution)/shard_map/ppermute | solution.py:385
  18.4 17.9 %collective-permute-start.6 = (bf16[20,128,128]{2,1,0:T(8,128)(2,1)S(1)}, bf16[20,128,128]{2,1,0:T(8,128)(2,1)S(1)}, u32[]{:S(2)}, u32[]{:S(2)}) collective-permute-start(bf16[20,128,128]{2,1,0:T(8,128)(2,1)S(1)} %get-tuple-element.45), channel_id=1, source_target_pairs={{8,0},{16,8},{24,16},{32,24},{40,32},{48,40},{56,48},{64,56},{72,6... | collective-permute-start | bytes 1966088 | tf_op jit(solution)/shard_map/ppermute | solution.py:386
  23.8 15.0 %copy-start = (bf16[56,128,128]{2,1,0:T(8,128)(2,1)}, bf16[56,128,128]{2,1,0:T(8,128)(2,1)S(1)}, u32[]{:S(2)}) copy-start(bf16[56,128,128]{2,1,0:T(8,128)(2,1)S(1)} %get-tuple-element.43.own_ref) | copy-start | bytes 5505028
  38.8 21.7 %collective-permute-start.7 = (f32[33,128,128]{2,1,0:T(8,128)}, f32[33,128,128]{2,1,0:T(8,128)}, u32[]{:S(2)}, u32[]{:S(2)}) collective-permute-start(f32[33,128,128]{2,1,0:T(8,128)} %products.7), channel_id=1, source_target_pairs={{0,1},{1,0},{2,3},{3,2},{4,5},{5,4},{6,7},{7,6},{8,9},{9,8},{10,11... | collective-permute-start | bytes 6488072 | tf_op jit(solution)/shard_map/ppermute | solution.py:355
  44.4 22.6 %all-to-all-start.1 = ((s32[64,1,128]{2,1,0:T(1,128)}), s32[64,1,128]{2,1,0:T(1,128)S(1)}, u32[]{:S(2)}, u32[]{:S(2)}) async-start(s32[64,1,128]{2,1,0:T(1,128)} %broadcast_in_dim.13), calls=%async_computation.1 | async-start | bytes 65536 | tf_op jit(solution)/shard_map/all_to_all | solution.py:387
  57.7 1.5 %copy-start.1 = (bf16[56,128,128]{2,1,0:T(8,128)(2,1)S(1)}, bf16[56,128,128]{2,1,0:T(8,128)(2,1)}, u32[]{:S(2)}) copy-start(bf16[56,128,128]{2,1,0:T(8,128)(2,1)} %copy-done) | copy-start | bytes 5505028
  64.4 17.4 %copy-start.2 = (s32[8]{0:T(128)S(1)}, s32[8]{0:T(128)}, u32[]{:S(2)}) copy-start(s32[8]{0:T(128)} %counts_ref.1) | copy-start | bytes 100
  64.4 21.9 %copy-start.4 = (bf16[8,7,128,128]{3,2,1,0:T(8,128)(2,1)S(1)}, bf16[8,7,128,128]{3,2,1,0:T(8,128)(2,1)}, u32[]{:S(2)}) copy-start(bf16[8,7,128,128]{3,2,1,0:T(8,128)(2,1)} %a_ref.1) | copy-start | bytes 5505028
  67.0 18.2 %all-to-all-start.2 = ((s16[4,1040,128]{2,1,0:T(8,128)(2,1)}), s16[4,1040,128]{2,1,0:T(8,128)(2,1)S(1)}, u32[]{:S(2)}, u32[]{:S(2)}) async-start(s16[4,1040,128]{2,1,0:T(8,128)(2,1)} %get-tuple-element.47), calls=%async_computation.2 | async-start | bytes 2129920 | tf_op jit(solution)/shard_map/all_to_all | solution.py:390
